TPU v7x, 32 devices: a whole 2x2x4 slice. The times are simulated.
32 devices in a mesh: slot: 2 (over x), region: 16 (over z, y, core).
Axes of the slice: x: 2, y: 2, z: 4, core: 2. Of those that a mesh axis runs over, the one named last changes fastest.
Arguments:
- ensemble: bfloat16 [4, 128, 512, 128], P('slot', 'region'), may hold values from -6 to 6
- observations: float32 [4, 128, 1024], P('slot', 'region'), may hold values from -12 to 12
- operator_weight: bfloat16 [1024, 512], replicated, may hold values from -0.25 to 0.25
- obs_precision: float32 [1024], replicated, may hold values from 0.02 to 0.2
- channel_mask: int32 [4, 1024], P('slot'), may hold values 0 or 1
Outputs:
- analysis: bfloat16 [4, 128, 512, 128], P('slot', 'region')
All inputs are finite; a program needn't handle non-finite values. No bound on the sum of `channel_mask` on one device may be relied on, other than what follows from the above.
Results may differ from a plain program's by a relative error of at most 0.014.
Values may be sent and summed in bfloat16 or wider, within the bound.
No kernel may reach another device: no remote copies, remote signals or barrier semaphores. Data moves between devices by JAX's collectives and lax.ppermute only.
A program may use at most 64 MiB of HBM per device.

v0:
```python
import functools
import math

import jax
import jax.numpy as jnp
from jax import lax
from jax.experimental import pallas as pl
from jax.experimental.pallas import tpu as pltpu
from jax.sharding import PartitionSpec as P

OUTER = 2
NS_STEPS = 8
NS_SPLIT = 4
LOCAL_WEIGHT = 0.5
F32 = jnp.float32
BF16 = jnp.bfloat16
VMEM_LIMIT = 28 * 1024 * 1024


def dot(a, b):
    return lax.dot_general(a, b, (((1,), (0,)), ((), ())), preferred_element_type=F32)


def dot_nt(a, b):
    return lax.dot_general(a, b, (((1,), (1,)), ((), ())), preferred_element_type=F32)


def split(x):
    hi = x.astype(BF16)
    return hi, (x - hi.astype(F32)).astype(BF16)


def cat(parts, axis):
    return jnp.concatenate(parts, axis=axis)


def iotas(m):
    return (
        lax.broadcasted_iota(jnp.int32, (m, m), 0),
        lax.broadcasted_iota(jnp.int32, (m, m), 1),
    )


def prepare(obs_ref, prec_ref, mask_ref, rw_ref, ow_ref):
    slots, patches, channels = obs_ref.shape
    members = rw_ref.shape[-1]
    pad = ow_ref.shape[0] - patches
    for t in range(slots):
        weight = prec_ref[...] * mask_ref[t : t + 1, :].astype(F32) / OUTER
        root = jnp.sqrt(weight)
        rw_ref[t] = jnp.broadcast_to(root, (members, channels)).T
        rows = (obs_ref[t] * root).astype(F32)
        if pad:
            rows = cat([rows, jnp.zeros((pad, channels), F32)], 0)
        ow_ref[:, t * channels : (t + 1) * channels] = rows.astype(BF16)


def quads(items, squash, w_ref, rw_ref, ow_ref, store, sq_s, x_s):
    slots, channels, members = rw_ref.shape

    def stage_a(i):
        for t in range(slots):
            sq_s[i, :, t * members : (t + 1) * members] = squash(items[i], t)

    def stage_b(i):
        predicted = dot(w_ref[...], sq_s[i])
        for t in range(slots):
            part = predicted[:, t * members : (t + 1) * members]
            x_s[i, t * channels : (t + 1) * channels, :] = (part * rw_ref[t]).astype(BF16)

    def stage_c(i):
        x = x_s[i]
        left = cat([x.T, ow_ref[...]], 0)
        both = dot(left, x)
        square = both[:members]
        tail = both[members:]
        rows = lax.broadcasted_iota(jnp.int32, tail.shape, 0)
        inner = jnp.sum(jnp.where(rows == items[i], tail, 0.0), axis=0, keepdims=True)
        scale = 1.0 / members
        row = jnp.sum(square, axis=0, keepdims=True) * scale
        col = jnp.sum(square, axis=1, keepdims=True) * scale
        total = jnp.sum(row, axis=1, keepdims=True) * scale
        diff = inner - row
        grad = diff - jnp.sum(diff, axis=1, keepdims=True) * scale
        store(items[i], square - row - (col - total), grad)

    n = len(items)
    for i in range(n + 2):
        if i < n:
            stage_a(i)
        if 0 <= i - 1 < n:
            stage_b(i - 1)
        if 0 <= i - 2 < n:
            stage_c(i - 2)


def edge_messages(odd, q_ref, qg_ref, far_ref, near_ref):
    last = q_ref.shape[0] - 1
    members = q_ref.shape[-1]
    pad = jnp.zeros((far_ref.shape[0] - members - 1, members), F32)
    low = cat([q_ref[0], qg_ref[0:1], pad], 0)
    high = cat([q_ref[last], qg_ref[last : last + 1], pad], 0)
    far_ref[...] = jnp.where(odd, high, low).astype(BF16)
    near_ref[...] = jnp.where(odd, low, high).astype(BF16)


def localize(odd, q_ref, qg_ref, far_ref, near_ref):
    patches, members = q_ref.shape[0], q_ref.shape[-1]
    far = far_ref[...].astype(F32)
    near = near_ref[...].astype(F32)
    left = jnp.where(odd, near, far)
    right = jnp.where(odd, far, near)
    grams = [left[:members]] + [q_ref[p] for p in range(patches)] + [right[:members]]
    grads = [left[members : members + 1]] + [qg_ref[p : p + 1] for p in range(patches)] + [right[members : members + 1]]
    mix = lambda v, p: v[p + 1] + LOCAL_WEIGHT * (v[p] + v[p + 2])
    return [mix(grams, p) for p in range(patches)], [mix(grads, p) for p in range(patches)]


def pack(grams, grads, out_ref):
    patches, members = len(grams), grams[0].shape[0]
    rid, cid = iotas(members)
    half = patches // 2
    rows = []
    for k in range(half):
        a, b = grams[k], grams[k + half]
        out_ref[k * members : (k + 1) * members] = jnp.where(rid <= cid, a, b).astype(BF16)
        rows.append(jnp.sum(jnp.where(rid == cid, b, 0.0), axis=0, keepdims=True))
    rows += list(grads)
    extra = out_ref.shape[0] - half * members
    rows.append(jnp.zeros((extra - len(rows), members), F32))
    out_ref[half * members :] = cat(rows, 0).astype(BF16)


def unpack(in_ref, patches):
    members = in_ref.shape[1]
    rid, cid = iotas(members)
    half = patches // 2
    rows = in_ref[half * members :].astype(F32)
    grams = [None] * patches
    for k in range(half):
        x = in_ref[k * members : (k + 1) * members].astype(F32)
        xt = x.T
        diag = rows[k : k + 1]
        grams[k] = jnp.where(rid <= cid, x, xt)
        grams[k + half] = jnp.where(rid > cid, x, jnp.where(rid < cid, xt, diag))
    return grams, [rows[half + p : half + p + 1] for p in range(patches)]


def inverse_roots(grams, grads):
    members = grams[0].shape[0]
    n = len(grams)
    every = range(n)
    rid, cid = iotas(members)
    identity = jnp.where(rid == cid, 1.0, 0.0).astype(F32)
    zero = jnp.zeros((members, members), BF16)
    shifted = [g + (members - 1.0) * identity for g in grams]
    square = [jnp.sum(jnp.sum(s * s, axis=0, keepdims=True), axis=1, keepdims=True) for s in shifted]
    norm = [jnp.sqrt(s) for s in square]
    t = [shifted[i] * (1.0 / norm[i]) for i in every]
    z = [None] * n
    for step in range(NS_SPLIT):
        sp = [split(v) for v in t]
        if step == 0:
            prod = [
                dot(cat([h, l], 1), cat([cat([h, l], 1), cat([h, zero], 1)], 0)) for h, l in sp
            ]
            sq = [v[:, :members] + v[:, members:] for v in prod]
            z = [1.5 * identity - 0.5 * v for v in t]
        else:
            zs = [split(v) for v in z]
            prod = []
            for (h, l), (zh, zl) in zip(sp, zs):
                top = cat([h, zh], 1)
                prod.append(dot(cat([h, l], 1), cat([top, top], 0)) + dot(h, cat([l, zl], 1)))
            sq = [v[:, :members] for v in prod]
            z = [1.5 * z[i] - 0.5 * prod[i][:, members:] for i in every]
        x = [split(1.5 * t[i] - 0.25 * sq[i]) for i in every]
        prod = [
            dot(cat([x[i][0], x[i][1]], 1), cat([cat(sp[i], 1), cat([sp[i][0], zero], 1)], 0))
            for i in every
        ]
        t = [2.25 * t[i] - (prod[i][:, :members] + prod[i][:, members:]) for i in every]
    d = [identity - v for v in t]
    for step in range(NS_SPLIT, NS_STEPS):
        dh = [v.astype(BF16) for v in d]
        if step < NS_STEPS - 1:
            prod = [dot(dh[i], cat([dh[i], z[i].astype(BF16)], 1)) for i in every]
            z = [z[i] + 0.5 * prod[i][:, members:] for i in every]
            d2 = [v[:, :members] for v in prod]
            d = [0.75 * d2[i] + 0.25 * dot(d2[i].astype(BF16), dh[i]) for i in every]
        else:
            z = [z[i] + 0.5 * dot(dh[i], z[i].astype(BF16)) for i in every]

    def rowdot(v, zs):
        h, l = split(jnp.broadcast_to(v, (8, members)))
        both = dot(cat([h, l], 1), cat([cat(zs, 1), cat([zs[0], zero], 1)], 0))
        return (both[:, :members] + both[:, members:])[0:1]

    zs = [split(v) for v in z]
    inner = [rowdot(grads[i], zs[i]) for i in every]
    along = [rowdot(inner[i], zs[i]) / norm[i] for i in every]
    scale = math.sqrt(members - 1.0)
    out = []
    for i in every:
        root = z[i] * (scale / jnp.sqrt(norm[i]))
        col = jnp.sum(root, axis=1, keepdims=True) * (1.0 / members)
        shift = along[i] - jnp.sum(along[i], axis=1, keepdims=True) * (1.0 / members) + 1.0 / members
        out.append((root - col) + shift)
    return out


def first_kernel(odd_ref, states_ref, w_ref, obs_ref, prec_ref, mask_ref,
                 q_ref, qg_ref, far_ref, near_ref, rw_ref, ow_ref, sq_s, x_s):
    prepare(obs_ref, prec_ref, mask_ref, rw_ref, ow_ref)

    def squash(p, t):
        return jnp.tanh(states_ref[t, p].astype(F32)).astype(BF16)

    def store(p, gram, grad):
        q_ref[p] = gram
        qg_ref[p : p + 1] = grad

    quads(list(range(q_ref.shape[0])), squash, w_ref, rw_ref, ow_ref, store, sq_s, x_s)
    edge_messages(odd_ref[0] == 1, q_ref, qg_ref, far_ref, near_ref)


def combine_kernel(odd_ref, q_ref, qg_ref, far_ref, near_ref, loc_ref, locg_ref, msg_ref):
    grams, grads = localize(odd_ref[0] == 1, q_ref, qg_ref, far_ref, near_ref)
    for p in range(len(grams)):
        loc_ref[p] = grams[p]
        locg_ref[p : p + 1] = grads[p]
    pack(grams, grads, msg_ref)


def totals(loc_ref, locg_ref, msg_ref):
    patches = loc_ref.shape[0]
    grams, grads = unpack(msg_ref, patches)
    return (
        [loc_ref[p] + grams[p] for p in range(patches)],
        [locg_ref[p : p + 1] + grads[p] for p in range(patches)],
    )


def moved(states, mixing):
    return dot_nt(states, mixing).astype(BF16)


def middle_kernel(odd_ref, loc_ref, locg_ref, msg_ref, states_ref, w_ref, rw_ref, ow_ref,
                  new_ref, q_ref, qg_ref, far_ref, near_ref, sq_s, x_s):
    mixing = [m.astype(BF16) for m in inverse_roots(*totals(loc_ref, locg_ref, msg_ref))]

    def squash(p, t):
        fresh = moved(states_ref[t, p], mixing[p])
        new_ref[t, p] = fresh
        return jnp.tanh(fresh.astype(F32)).astype(BF16)

    def store(p, gram, grad):
        q_ref[p] = gram
        qg_ref[p : p + 1] = grad

    quads(list(range(q_ref.shape[0])), squash, w_ref, rw_ref, ow_ref, store, sq_s, x_s)
    edge_messages(odd_ref[0] == 1, q_ref, qg_ref, far_ref, near_ref)


def last_kernel(loc_ref, locg_ref, msg_ref, states_ref, out_ref):
    mixing = [m.astype(BF16) for m in inverse_roots(*totals(loc_ref, locg_ref, msg_ref))]
    slots, patches = states_ref.shape[:2]
    for p in range(patches):
        for t in range(slots):
            out_ref[t, p] = moved(states_ref[t, p], mixing[p])


def call(kernel, out_shape, args, scratch=(), smem=True):
    vmem = pl.BlockSpec(memory_space=pltpu.VMEM)
    specs = [vmem] * len(args)
    if smem:
        specs[0] = pl.BlockSpec(memory_space=pltpu.SMEM)
    outs = [jax.ShapeDtypeStruct(s, d) for s, d in out_shape]
    return pl.pallas_call(
        kernel,
        out_shape=outs,
        in_specs=specs,
        out_specs=[vmem] * len(outs),
        scratch_shapes=[pltpu.VMEM(s, d) for s, d in scratch],
        compiler_params=pltpu.CompilerParams(vmem_limit_bytes=VMEM_LIMIT),
    )(*args)


def neighbours(far, near):
    count = lax.axis_size("region")
    mate = [(r, r ^ 1) for r in range(count)]
    cross = [(r, (r + 1) % count if r % 2 else (r - 1) % count) for r in range(count)]
    return lax.ppermute(far, "region", cross), lax.ppermute(near, "region", mate)


def over_slots(msg):
    count = lax.axis_size("slot")
    if count == 2:
        return lax.ppermute(msg, "slot", [(0, 1), (1, 0)])
    mine = msg.astype(F32)
    return (lax.psum(mine, "slot") - mine).astype(BF16)


def shards(ensemble, observations, operator_weight, obs_precision, channel_mask):
    slots, patches, rows, members = ensemble.shape
    channels = operator_weight.shape[0]
    if lax.axis_size("region") % 2 or patches % 2 or patches > 16:
        raise ValueError("unsupported split")
    odd = (lax.axis_index("region") % 2).astype(jnp.int32).reshape(1)
    edge = ((members + 16, members), BF16)
    q = ((patches, members, members), F32)
    qg = ((patches, members), F32)
    extra = -(-(patches // 2 + patches) // 16) * 16
    msg_shape = ((patches // 2 * members + extra, members), BF16)
    scratch = (
        ((patches, rows, slots * members), BF16),
        ((patches, slots * channels, members), BF16),
    )
    rw = ((slots, channels, members), F32)
    ow = ((16, slots * channels), BF16)
    out = (ensemble.shape, BF16)

    gram, grad, far, near, root_w, obs_w = call(
        first_kernel,
        [q, qg, edge, edge, rw, ow],
        (odd, ensemble, operator_weight, observations, obs_precision[None, :], channel_mask),
        scratch,
    )
    states = ensemble
    for step in range(OUTER):
        far, near = neighbours(far, near)
        loc, locg, msg = call(combine_kernel, [q, qg, msg_shape], (odd, gram, grad, far, near))
        msg = over_slots(msg)
        if step < OUTER - 1:
            states, gram, grad, far, near = call(
                middle_kernel,
                [out, q, qg, edge, edge],
                (odd, loc, locg, msg, states, operator_weight, root_w, obs_w),
                scratch,
            )
        else:
            states = call(last_kernel, [out], (loc, locg, msg, states), smem=False)[0]
    return states


def solution(mesh):
    return jax.shard_map(
        shards,
        mesh=mesh,
        in_specs=(
            P("slot", "region", None, None),
            P("slot", "region", None),
            P(),
            P(),
            P("slot", None),
        ),
        out_specs=P("slot", "region", None, None),
        check_vma=False,
    )
```

profile of v0, /device:TPU:0, one launch (start us, length us, event | category | flops | bytes accessed | tf_op | source)
XLA Modules:
  0.0 48.4 jit_solution(8803289850515611556)
XLA Ops:
  0.0 0.0 copy-start
  0.0 1.6 %copy-done = bf16[2,8,512,128]{3,2,1,0:T(8,128)(2,1)S(1)} copy-done((bf16[2,8,512,128]{3,2,1,0:T(8,128)(2,1)S(1)}, bf16[2,8,512,128]{3,2,1,0:T(8,128)(2,1)}, u32[]{:S(2)}) %copy-start) | copy-done | bytes 2097176
  1.6 1.2 %copy-done.2 = bf16[1024,512]{1,0:T(8,128)(2,1)S(1)} copy-done((bf16[1024,512]{1,0:T(8,128)(2,1)S(1)}, bf16[1024,512]{1,0:T(8,128)(2,1)}, u32[]{:S(2)}) %copy-start.2) | copy-done | bytes 1048600
  2.8 0.8 %copy-done.3 = f32[2,8,1024]{2,1,0:T(8,128)S(1)} copy-done((f32[2,8,1024]{2,1,0:T(8,128)S(1)}, f32[2,8,1024]{2,1,0:T(8,128)}, u32[]{:S(2)}) %copy-start.3) | copy-done | bytes 65560
  3.7 0.7 %copy-done.4 = s32[2,1024]{1,0:T(2,128)S(1)} copy-done((s32[2,1024]{1,0:T(2,128)S(1)}, s32[2,1024]{1,0:T(2,128)}, u32[]{:S(2)}) %copy-start.4) | copy-done | bytes 8216
  4.4 0.7 %copy-done.5 = f32[1024]{0:T(1024)S(1)} copy-done((f32[1024]{0:T(1024)S(1)}, f32[1024]{0:T(1024)}, u32[]{:S(2)}) %copy-start.5) | copy-done | bytes 4120
  5.0 5.0 %shard_map.55 = (f32[8,128,128]{2,1,0:T(8,128)S(1)}, f32[8,128]{1,0:T(8,128)S(1)}, bf16[144,128]{1,0:T(8,128)(2,1)S(1)}, bf16[144,128]{1,0:T(8,128)(2,1)S(1)}, f...) custom-call(s32[1]{0:T(128)} %bitcast.odd_ref, bf16[2,8,512,128]{3,2,1,0:T(8,128)(2,1)S(1)} %copy-done, ...), custom_call_target="tpu_custom_call" | custom-call | tf_op jit(solution)/shard_map/pallas_call | solution.py:279
  10.0 5.5 %collective-permute-start = (bf16[144,128]{1,0:T(8,128)(2,1)S(1)}, bf16[144,128]{1,0:T(8,128)(2,1)S(1)}, u32[]{:S(2)}, u32[]{:S(2)}) collective-permute-start(bf16[144,128]{1,0:T(8,128)(2,1)S(1)} %get-tuple-element.24), channel_id=1, source_target_pairs={{0,15},{1,2},{2,1},{3,4},{4,3},{5,6},{6,5},{7,8},{8,7},{9,10},{10,... | collective-permute-start | bytes 110600 | tf_op jit(solution)/shard_map/ppermute | solution.py:293
  15.6 0.0 collective-permute-start.1
  15.6 1.6 %collective-permute-done.far_ref = bf16[144,128]{1,0:T(8,128)(2,1)S(1)} collective-permute-done((bf16[144,128]{1,0:T(8,128)(2,1)S(1)}, bf16[144,128]{1,0:T(8,128)(2,1)S(1)}, u32[]{:S(2)}, u32[]{:S(2)}) %collective-permute-start) | collective-permute-done | bytes 36896 | tf_op jit(solution)/shard_map/ppermute | solution.py:293
  17.2 0.0 collective-permute-done.1.near_ref
  17.2 0.1 shard_map.56
  17.4 2.0 %collective-permute-start.2 = (bf16[528,128]{1,0:T(8,128)(2,1)S(1)}, bf16[528,128]{1,0:T(8,128)(2,1)S(1)}, u32[]{:S(2)}, u32[]{:S(2)}) collective-permute-start(bf16[528,128]{1,0:T(8,128)(2,1)S(1)} %get-tuple-element.28), channel_id=1, source_target_pairs={{0,16},{16,0},{1,17},{17,1},{2,18},{18,2},{3,19},{19,3},{4,20},{20... | collective-permute-start | bytes 405512 | tf_op jit(solution)/shard_map/ppermute | solution.py:299
  19.4 3.3 %collective-permute-done.2.msg_ref = bf16[528,128]{1,0:T(8,128)(2,1)S(1)} collective-permute-done((bf16[528,128]{1,0:T(8,128)(2,1)S(1)}, bf16[528,128]{1,0:T(8,128)(2,1)S(1)}, u32[]{:S(2)}, u32[]{:S(2)}) %collective-permute-start.2) | collective-permute-done | bytes 135200 | tf_op jit(solution)/shard_map/ppermute | solution.py:299
  22.6 0.0 copy-done.1
  22.6 8.9 %shard_map.57 = (bf16[2,8,512,128]{3,2,1,0:T(8,128)(2,1)S(1)}, f32[8,128,128]{2,1,0:T(8,128)S(1)}, f32[8,128]{1,0:T(8,128)S(1)}, bf16[144,128]{1,0:T(8,128)(2,1)S(1)}, bf16[144,128]{1,0:T(8,128)(2,1)S(1)}) custom-call(s32[1]{0:T(128)} %bitcast.odd_ref, f32[8,128,128]{2,1,0:T(8,128)S(1)} %get-tuple-element.26.loc_ref, ...), custom_call_target="tpu_custom_call" | custom-call | tf_op jit(solution)/shard_map/pallas_call | solution.py:279
  31.6 3.1 %collective-permute-start.3 = (bf16[144,128]{1,0:T(8,128)(2,1)S(1)}, bf16[144,128]{1,0:T(8,128)(2,1)S(1)}, u32[]{:S(2)}, u32[]{:S(2)}) collective-permute-start(bf16[144,128]{1,0:T(8,128)(2,1)S(1)} %get-tuple-element.33), channel_id=1, source_target_pairs={{0,15},{1,2},{2,1},{3,4},{4,3},{5,6},{6,5},{7,8},{8,7},{9,10},{10,... | collective-permute-start | bytes 110600 | tf_op jit(solution)/shard_map/ppermute | solution.py:293
  34.7 0.0 collective-permute-start.4
  34.7 3.0 %collective-permute-done.3.far_ref = bf16[144,128]{1,0:T(8,128)(2,1)S(1)} collective-permute-done((bf16[144,128]{1,0:T(8,128)(2,1)S(1)}, bf16[144,128]{1,0:T(8,128)(2,1)S(1)}, u32[]{:S(2)}, u32[]{:S(2)}) %collective-permute-start.3) | collective-permute-done | bytes 36896 | tf_op jit(solution)/shard_map/ppermute | solution.py:293
  37.7 0.0 collective-permute-done.4.near_ref
  37.7 0.1 shard_map.58
  37.9 1.8 %collective-permute-start.5 = (bf16[528,128]{1,0:T(8,128)(2,1)S(1)}, bf16[528,128]{1,0:T(8,128)(2,1)S(1)}, u32[]{:S(2)}, u32[]{:S(2)}) collective-permute-start(bf16[528,128]{1,0:T(8,128)(2,1)S(1)} %get-tuple-element.37), channel_id=1, source_target_pairs={{0,16},{16,0},{1,17},{17,1},{2,18},{18,2},{3,19},{19,3},{4,20},{20... | collective-permute-start | bytes 405512 | tf_op jit(solution)/shard_map/ppermute | solution.py:299
  39.6 3.3 %collective-permute-done.5.msg_ref = bf16[528,128]{1,0:T(8,128)(2,1)S(1)} collective-permute-done((bf16[528,128]{1,0:T(8,128)(2,1)S(1)}, bf16[528,128]{1,0:T(8,128)(2,1)S(1)}, u32[]{:S(2)}, u32[]{:S(2)}) %collective-permute-start.5) | collective-permute-done | bytes 135200 | tf_op jit(solution)/shard_map/ppermute | solution.py:299
  42.9 5.4 %shard_map.59 = bf16[2,8,512,128]{3,2,1,0:T(8,128)(2,1)} custom-call(f32[8,128,128]{2,1,0:T(8,128)S(1)} %get-tuple-element.35.loc_ref, f32[8,128]{1,0:T(8,128)S(1)} %get-tuple-element.36.locg_ref, bf16[528,128]{1,0:T(8,128)(2,1)S(1)} %collective-permute-done.5.msg_ref, bf16[2,8,512,128]{3,2,1,0:T(8,128)(2,1)S(1)} %get-tuple-element.38.states_ref), custom_call_target="tpu_custom_call" | custom-call | tf_op jit(solution)/shard_map/pallas_call | solution.py:279
  (5 shorter events, 0.0 us)
Async XLA Ops:
  0.0 1.6 %copy-start = (bf16[2,8,512,128]{3,2,1,0:T(8,128)(2,1)S(1)}, bf16[2,8,512,128]{3,2,1,0:T(8,128)(2,1)}, u32[]{:S(2)}) copy-start(bf16[2,8,512,128]{3,2,1,0:T(8,128)(2,1)} %states_ref.3) | copy-start | bytes 6291460
  1.6 1.2 %copy-start.2 = (bf16[1024,512]{1,0:T(8,128)(2,1)S(1)}, bf16[1024,512]{1,0:T(8,128)(2,1)}, u32[]{:S(2)}) copy-start(bf16[1024,512]{1,0:T(8,128)(2,1)} %w_ref.3) | copy-start | bytes 3145732
  2.8 0.8 %copy-start.3 = (f32[2,8,1024]{2,1,0:T(8,128)S(1)}, f32[2,8,1024]{2,1,0:T(8,128)}, u32[]{:S(2)}) copy-start(f32[2,8,1024]{2,1,0:T(8,128)} %obs_ref.1) | copy-start | bytes 196612
  3.7 0.7 %copy-start.4 = (s32[2,1024]{1,0:T(2,128)S(1)}, s32[2,1024]{1,0:T(2,128)}, u32[]{:S(2)}) copy-start(s32[2,1024]{1,0:T(2,128)} %mask_ref.1) | copy-start | bytes 24580
  4.4 0.7 %copy-start.5 = (f32[1024]{0:T(1024)S(1)}, f32[1024]{0:T(1024)}, u32[]{:S(2)}) copy-start(f32[1024]{0:T(1024)} %param.8) | copy-start | bytes 12292
  5.0 17.6 %copy-start.1 = (bf16[2,8,512,128]{3,2,1,0:T(8,128)(2,1)S(1)}, bf16[2,8,512,128]{3,2,1,0:T(8,128)(2,1)}, u32[]{:S(2)}) copy-start(bf16[2,8,512,128]{3,2,1,0:T(8,128)(2,1)} %states_ref.3) | copy-start | bytes 6291460
  10.0 7.2 %collective-permute-start = (bf16[144,128]{1,0:T(8,128)(2,1)S(1)}, bf16[144,128]{1,0:T(8,128)(2,1)S(1)}, u32[]{:S(2)}, u32[]{:S(2)}) collective-permute-start(bf16[144,128]{1,0:T(8,128)(2,1)S(1)} %get-tuple-element.24), channel_id=1, source_target_pairs={{0,15},{1,2},{2,1},{3,4},{4,3},{5,6},{6,5},{7,8},{8,7},{9,10},{10,... | collective-permute-start | bytes 110600 | tf_op jit(solution)/shard_map/ppermute | solution.py:293
  15.6 1.6 %collective-permute-start.1 = (bf16[144,128]{1,0:T(8,128)(2,1)S(1)}, bf16[144,128]{1,0:T(8,128)(2,1)S(1)}, u32[]{:S(2)}, u32[]{:S(2)}) collective-permute-start(bf16[144,128]{1,0:T(8,128)(2,1)S(1)} %get-tuple-element.25), channel_id=1, source_target_pairs={{0,1},{1,0},{2,3},{3,2},{4,5},{5,4},{6,7},{7,6},{8,9},{9,8},{10,11... | collective-permute-start | bytes 110600 | tf_op jit(solution)/shard_map/ppermute | solution.py:293
  17.4 5.3 %collective-permute-start.2 = (bf16[528,128]{1,0:T(8,128)(2,1)S(1)}, bf16[528,128]{1,0:T(8,128)(2,1)S(1)}, u32[]{:S(2)}, u32[]{:S(2)}) collective-permute-start(bf16[528,128]{1,0:T(8,128)(2,1)S(1)} %get-tuple-element.28), channel_id=1, source_target_pairs={{0,16},{16,0},{1,17},{17,1},{2,18},{18,2},{3,19},{19,3},{4,20},{20... | collective-permute-start | bytes 405512 | tf_op jit(solution)/shard_map/ppermute | solution.py:299
  31.6 6.1 %collective-permute-start.3 = (bf16[144,128]{1,0:T(8,128)(2,1)S(1)}, bf16[144,128]{1,0:T(8,128)(2,1)S(1)}, u32[]{:S(2)}, u32[]{:S(2)}) collective-permute-start(bf16[144,128]{1,0:T(8,128)(2,1)S(1)} %get-tuple-element.33), channel_id=1, source_target_pairs={{0,15},{1,2},{2,1},{3,4},{4,3},{5,6},{6,5},{7,8},{8,7},{9,10},{10,... | collective-permute-start | bytes 110600 | tf_op jit(solution)/shard_map/ppermute | solution.py:293
  34.7 3.0 %collective-permute-start.4 = (bf16[144,128]{1,0:T(8,128)(2,1)S(1)}, bf16[144,128]{1,0:T(8,128)(2,1)S(1)}, u32[]{:S(2)}, u32[]{:S(2)}) collective-permute-start(bf16[144,128]{1,0:T(8,128)(2,1)S(1)} %get-tuple-element.34), channel_id=1, source_target_pairs={{0,1},{1,0},{2,3},{3,2},{4,5},{5,4},{6,7},{7,6},{8,9},{9,8},{10,11... | collective-permute-start | bytes 110600 | tf_op jit(solution)/shard_map/ppermute | solution.py:293
  37.9 5.1 %collective-permute-start.5 = (bf16[528,128]{1,0:T(8,128)(2,1)S(1)}, bf16[528,128]{1,0:T(8,128)(2,1)S(1)}, u32[]{:S(2)}, u32[]{:S(2)}) collective-permute-start(bf16[528,128]{1,0:T(8,128)(2,1)S(1)} %get-tuple-element.37), channel_id=1, source_target_pairs={{0,16},{16,0},{1,17},{17,1},{2,18},{18,2},{3,19},{19,3},{4,20},{20... | collective-permute-start | bytes 405512 | tf_op jit(solution)/shard_map/ppermute | solution.py:299
where the time goes:
time: 48.7 us; the launch traced here: 48.4 us
  Pallas kernels  19.6 us (40%)
  starting transfers between devices  12.5 us (26%)
  waiting for transfers between devices  11.2 us (23%)
  local copies, waits for them, and re-layouts  5.04 us (10%)
    pallas_call x5, Pallas kernels, call(): pl.pallas_call(kernel, out_shape=outs, in_specs=specs, out_specs=[vmem] *...  19.6 us
    ppermute x2, starting transfers between devices, neighbours(): lax.ppermute(far, 'region', cross)  8.69 us
    ppermute x2, waiting for transfers between devices, over_slots(): return lax.ppermute(msg, 'slot', [(0, 1), (1, 0)])  6.56 us
    unnamed x12, local copies, waits for them, and re-layouts  5.04 us
    ppermute x2, waiting for transfers between devices, neighbours(): lax.ppermute(far, 'region', cross)  4.63 us
    ppermute x2, starting transfers between devices, over_slots(): return lax.ppermute(msg, 'slot', [(0, 1), (1, 0)])  3.8 us
  transfers between devices with their start and end apart: 6, of which 4 were waited for; matrix products, arithmetic and copies ran while one was open for 0% of the time, Pallas kernels for 0%

commit v1 on v0

--- a/solution.py
+++ b/solution.py
@@ -94,26 +94,29 @@
             stage_c(i - 2)
 
 
-def edge_messages(odd, q_ref, qg_ref, far_ref, near_ref):
-    last = q_ref.shape[0] - 1
-    members = q_ref.shape[-1]
+def edges_of(odd, low, high, far_ref, near_ref):
+    members = low[0].shape[0]
     pad = jnp.zeros((far_ref.shape[0] - members - 1, members), F32)
-    low = cat([q_ref[0], qg_ref[0:1], pad], 0)
-    high = cat([q_ref[last], qg_ref[last : last + 1], pad], 0)
+    low = cat([low[0], low[1], pad], 0)
+    high = cat([high[0], high[1], pad], 0)
     far_ref[...] = jnp.where(odd, high, low).astype(BF16)
     near_ref[...] = jnp.where(odd, low, high).astype(BF16)
 
 
-def localize(odd, q_ref, qg_ref, far_ref, near_ref):
-    patches, members = q_ref.shape[0], q_ref.shape[-1]
+def localize(odd, edge_refs, inner_refs, far_ref, near_ref):
+    q_edge, qg_edge = edge_refs
+    q_inner, qg_inner = inner_refs
+    members = q_edge.shape[-1]
     far = far_ref[...].astype(F32)
     near = near_ref[...].astype(F32)
     left = jnp.where(odd, near, far)
     right = jnp.where(odd, far, near)
-    grams = [left[:members]] + [q_ref[p] for p in range(patches)] + [right[:members]]
-    grads = [left[members : members + 1]] + [qg_ref[p : p + 1] for p in range(patches)] + [right[members : members + 1]]
+    inner = q_inner.shape[0]
+    grams = [left[:members], q_edge[0]] + [q_inner[p] for p in range(inner)] + [q_edge[1], right[:members]]
+    tail = slice(members, members + 1)
+    grads = [left[tail], qg_edge[0:1]] + [qg_inner[p : p + 1] for p in range(inner)] + [qg_edge[1:2], right[tail]]
     mix = lambda v, p: v[p + 1] + LOCAL_WEIGHT * (v[p] + v[p + 2])
-    return [mix(grams, p) for p in range(patches)], [mix(grads, p) for p in range(patches)]
+    return [mix(grams, p) for p in range(inner + 2)], [mix(grads, p) for p in range(inner + 2)]
 
 
 def pack(grams, grads, out_ref):
@@ -209,23 +212,82 @@
     return out
 
 
-def first_kernel(odd_ref, states_ref, w_ref, obs_ref, prec_ref, mask_ref,
-                 q_ref, qg_ref, far_ref, near_ref, rw_ref, ow_ref, sq_s, x_s):
-    prepare(obs_ref, prec_ref, mask_ref, rw_ref, ow_ref)
-
+def squash_of(states_ref):
+    return lambda p, t: jnp.tanh(states_ref[t, p].astype(F32)).astype(BF16)
+
+
+def advance(states_ref, mixing_of, new_ref):
     def squash(p, t):
-        return jnp.tanh(states_ref[t, p].astype(F32)).astype(BF16)
-
+        fresh = dot_nt(states_ref[t, p], mixing_of(p)).astype(BF16)
+        new_ref[t, p] = fresh
+        return jnp.tanh(fresh.astype(F32)).astype(BF16)
+
+    return squash
+
+
+def into(q_ref, qg_ref, first):
     def store(p, gram, grad):
-        q_ref[p] = gram
-        qg_ref[p : p + 1] = grad
-
-    quads(list(range(q_ref.shape[0])), squash, w_ref, rw_ref, ow_ref, store, sq_s, x_s)
-    edge_messages(odd_ref[0] == 1, q_ref, qg_ref, far_ref, near_ref)
-
-
-def combine_kernel(odd_ref, q_ref, qg_ref, far_ref, near_ref, loc_ref, locg_ref, msg_ref):
-    grams, grads = localize(odd_ref[0] == 1, q_ref, qg_ref, far_ref, near_ref)
+        q_ref[p - first] = gram
+        qg_ref[p - first : p - first + 1] = grad
+
+    return store
+
+
+def edge_quads(odd, patches, squash, w_ref, rw_ref, ow_ref, q_ref, qg_ref, far_ref, near_ref, sq_s, x_s):
+    ends = [0, patches - 1]
+    found = {}
+
+    def store(p, gram, grad):
+        found[p] = (gram, grad)
+        k = ends.index(p)
+        q_ref[k] = gram
+        qg_ref[k : k + 1] = grad
+
+    quads(ends, squash, w_ref, rw_ref, ow_ref, store, sq_s, x_s)
+    edges_of(odd, found[ends[0]], found[ends[1]], far_ref, near_ref)
+
+
+def first_kernel(odd_ref, states_hbm, w_hbm, obs_hbm, prec_hbm, mask_hbm,
+                 states_ref, w_ref, q_ref, qg_ref, far_ref, near_ref, rw_ref, ow_ref,
+                 sq_s, x_s, obs_s, prec_s, mask_s, sems):
+    patches = states_ref.shape[1]
+    slots = states_ref.shape[0]
+    ends = [0, patches - 1]
+    small = [
+        pltpu.make_async_copy(prec_hbm, prec_s, sems.at[0]),
+        pltpu.make_async_copy(mask_hbm, mask_s, sems.at[1]),
+        pltpu.make_async_copy(obs_hbm, obs_s, sems.at[2]),
+    ]
+    weights = pltpu.make_async_copy(w_hbm, w_ref, sems.at[3])
+    state = {
+        (t, p): pltpu.make_async_copy(
+            states_hbm.at[t, p], states_ref.at[t, p], sems.at[4 + t * patches + p]
+        )
+        for p in range(patches)
+        for t in range(slots)
+    }
+    early = [state[t, p] for p in ends for t in range(slots)]
+    for c in early + [weights] + small:
+        c.start()
+    late = [state[t, p] for p in range(1, patches - 1) for t in range(slots)]
+    for c in late:
+        c.start()
+    for c in early + [weights] + small:
+        c.wait()
+    prepare(obs_s, prec_s, mask_s, rw_ref, ow_ref)
+    edge_quads(odd_ref[0] == 1, patches, squash_of(states_ref), w_ref, rw_ref, ow_ref,
+               q_ref, qg_ref, far_ref, near_ref, sq_s, x_s)
+    for c in late:
+        c.wait()
+
+
+def inner_kernel(states_ref, w_ref, rw_ref, ow_ref, q_ref, qg_ref, sq_s, x_s):
+    items = list(range(1, states_ref.shape[1] - 1))
+    quads(items, squash_of(states_ref), w_ref, rw_ref, ow_ref, into(q_ref, qg_ref, 1), sq_s, x_s)
+
+
+def combine_kernel(odd_ref, qe_ref, qge_ref, qi_ref, qgi_ref, far_ref, near_ref, loc_ref, locg_ref, msg_ref):
+    grams, grads = localize(odd_ref[0] == 1, (qe_ref, qge_ref), (qi_ref, qgi_ref), far_ref, near_ref)
     for p in range(len(grams)):
         loc_ref[p] = grams[p]
         locg_ref[p : p + 1] = grads[p]
@@ -241,48 +303,67 @@
     )
 
 
-def moved(states, mixing):
-    return dot_nt(states, mixing).astype(BF16)
-
-
-def middle_kernel(odd_ref, loc_ref, locg_ref, msg_ref, states_ref, w_ref, rw_ref, ow_ref,
-                  new_ref, q_ref, qg_ref, far_ref, near_ref, sq_s, x_s):
+def root_kernel(odd_ref, loc_ref, locg_ref, msg_ref, states_ref, w_ref, rw_ref, ow_ref,
+                mix_ref, new_ref, q_ref, qg_ref, far_ref, near_ref, sq_s, x_s):
     mixing = [m.astype(BF16) for m in inverse_roots(*totals(loc_ref, locg_ref, msg_ref))]
-
-    def squash(p, t):
-        fresh = moved(states_ref[t, p], mixing[p])
-        new_ref[t, p] = fresh
-        return jnp.tanh(fresh.astype(F32)).astype(BF16)
-
-    def store(p, gram, grad):
-        q_ref[p] = gram
-        qg_ref[p : p + 1] = grad
-
-    quads(list(range(q_ref.shape[0])), squash, w_ref, rw_ref, ow_ref, store, sq_s, x_s)
-    edge_messages(odd_ref[0] == 1, q_ref, qg_ref, far_ref, near_ref)
-
-
-def last_kernel(loc_ref, locg_ref, msg_ref, states_ref, out_ref):
+    patches = loc_ref.shape[0]
+    for p in range(1, patches - 1):
+        mix_ref[p - 1] = mixing[p]
+    ends = [0, patches - 1]
+    place = lambda ref: _Placed(ref, ends)
+    edge_quads(odd_ref[0] == 1, patches, advance(states_ref, lambda p: mixing[p], place(new_ref)),
+               w_ref, rw_ref, ow_ref, q_ref, qg_ref, far_ref, near_ref, sq_s, x_s)
+
+
+class _Placed:
+    def __init__(self, ref, items):
+        self.ref, self.items = ref, items
+
+    def __setitem__(self, where, value):
+        self.ref[where[0], self.items.index(where[1])] = value
+
+
+def advance_kernel(mix_ref, states_ref, w_ref, rw_ref, ow_ref, new_ref, q_ref, qg_ref, sq_s, x_s):
+    items = list(range(1, states_ref.shape[1] - 1))
+    squash = advance(states_ref, lambda p: mix_ref[p - 1], _Placed(new_ref, items))
+    quads(items, squash, w_ref, rw_ref, ow_ref, into(q_ref, qg_ref, 1), sq_s, x_s)
+
+
+def last_kernel(loc_ref, locg_ref, msg_ref, *refs):
+    *states, out_hbm, out_s, sems = refs
     mixing = [m.astype(BF16) for m in inverse_roots(*totals(loc_ref, locg_ref, msg_ref))]
-    slots, patches = states_ref.shape[:2]
+    slots, patches = out_s.shape[:2]
+    copies = []
     for p in range(patches):
         for t in range(slots):
-            out_ref[t, p] = moved(states_ref[t, p], mixing[p])
-
-
-def call(kernel, out_shape, args, scratch=(), smem=True):
-    vmem = pl.BlockSpec(memory_space=pltpu.VMEM)
-    specs = [vmem] * len(args)
-    if smem:
-        specs[0] = pl.BlockSpec(memory_space=pltpu.SMEM)
+            if len(states) == 1:
+                value = states[0][t, p]
+            elif p in (0, patches - 1):
+                value = states[0][t, min(p, 1)]
+            else:
+                value = states[1][t, p - 1]
+            out_s[t, p] = dot_nt(value, mixing[p]).astype(BF16)
+            copies.append(pltpu.make_async_copy(out_s.at[t, p], out_hbm.at[t, p], sems.at[len(copies)]))
+            copies[-1].start()
+    for c in copies:
+        c.wait()
+
+
+SPACES = {"s": pltpu.SMEM, "v": pltpu.VMEM, "h": pltpu.HBM}
+
+
+def call(kernel, out_shape, args, kinds, scratch=(), flops=10 ** 9, out_kinds=None):
     outs = [jax.ShapeDtypeStruct(s, d) for s, d in out_shape]
+    spec = lambda k: pl.BlockSpec(memory_space=SPACES[k])
     return pl.pallas_call(
         kernel,
         out_shape=outs,
-        in_specs=specs,
-        out_specs=[vmem] * len(outs),
-        scratch_shapes=[pltpu.VMEM(s, d) for s, d in scratch],
+        in_specs=[spec(k) for k in kinds],
+        out_specs=[spec(k) for k in (out_kinds or "v" * len(outs))],
+        scratch_shapes=[pltpu.VMEM(*s) if isinstance(s, tuple) else s for s in scratch],
+        cost_estimate=pl.CostEstimate(flops=flops, bytes_accessed=0, transcendentals=0),
         compiler_params=pltpu.CompilerParams(vmem_limit_bytes=VMEM_LIMIT),
+        name=kernel.__name__,
     )(*args)
 
 
@@ -304,43 +385,80 @@
 def shards(ensemble, observations, operator_weight, obs_precision, channel_mask):
     slots, patches, rows, members = ensemble.shape
     channels = operator_weight.shape[0]
-    if lax.axis_size("region") % 2 or patches % 2 or patches > 16:
+    if lax.axis_size("region") % 2 or patches % 2 or not 4 <= patches <= 16:
         raise ValueError("unsupported split")
+    inner = patches - 2
     odd = (lax.axis_index("region") % 2).astype(jnp.int32).reshape(1)
     edge = ((members + 16, members), BF16)
-    q = ((patches, members, members), F32)
-    qg = ((patches, members), F32)
+    gram = lambda n: ((n, members, members), F32)
+    grad = lambda n: ((n, members), F32)
     extra = -(-(patches // 2 + patches) // 16) * 16
     msg_shape = ((patches // 2 * members + extra, members), BF16)
-    scratch = (
-        ((patches, rows, slots * members), BF16),
-        ((patches, slots * channels, members), BF16),
+    scratch = lambda n: (
+        ((n, rows, slots * members), BF16),
+        ((n, slots * channels, members), BF16),
     )
     rw = ((slots, channels, members), F32)
     ow = ((16, slots * channels), BF16)
-    out = (ensemble.shape, BF16)
-
-    gram, grad, far, near, root_w, obs_w = call(
+    state = lambda n: ((slots, n, rows, members), BF16)
+    prec = obs_precision[None, :]
+    dma = pltpu.SemaphoreType.DMA
+    hbm = lambda x: pltpu.with_memory_space_constraint(x, pltpu.HBM)
+
+    states, weight, qe, qge, far, near, root_w, obs_w = call(
         first_kernel,
-        [q, qg, edge, edge, rw, ow],
-        (odd, ensemble, operator_weight, observations, obs_precision[None, :], channel_mask),
-        scratch,
-    )
-    states = ensemble
+        [state(patches), (operator_weight.shape, BF16), gram(2), grad(2), edge, edge, rw, ow],
+        (odd, hbm(ensemble), hbm(operator_weight), hbm(observations), hbm(prec), hbm(channel_mask)),
+        "shhhhh",
+        scratch(2) + (
+            (observations.shape, F32),
+            (prec.shape, F32),
+            (channel_mask.shape, jnp.int32),
+            dma((4 + slots * patches,)),
+        ),
+    )
+    far, near = neighbours(far, near)
+    qi, qgi = call(
+        inner_kernel, [gram(inner), grad(inner)], (states, weight, root_w, obs_w), "vvvv", scratch(inner)
+    )
+    parts = (states,)
     for step in range(OUTER):
+        loc, locg, msg = call(
+            combine_kernel,
+            [gram(patches), grad(patches), msg_shape],
+            (odd, qe, qge, qi, qgi, far, near),
+            "svvvvvv",
+        )
+        msg = over_slots(msg)
+        if step == OUTER - 1:
+            break
+        if len(parts) > 1:
+            edges, inside = parts
+            states = jnp.concatenate([edges[:, :1], inside, edges[:, 1:]], axis=1)
+        mix, edges, qe, qge, far, near = call(
+            root_kernel,
+            [((inner, members, members), BF16), state(2), gram(2), grad(2), edge, edge],
+            (odd, loc, locg, msg, states, weight, root_w, obs_w),
+            "svvvvvvv",
+            scratch(2),
+        )
         far, near = neighbours(far, near)
-        loc, locg, msg = call(combine_kernel, [q, qg, msg_shape], (odd, gram, grad, far, near))
-        msg = over_slots(msg)
-        if step < OUTER - 1:
-            states, gram, grad, far, near = call(
-                middle_kernel,
-                [out, q, qg, edge, edge],
-                (odd, loc, locg, msg, states, operator_weight, root_w, obs_w),
-                scratch,
-            )
-        else:
-            states = call(last_kernel, [out], (loc, locg, msg, states), smem=False)[0]
-    return states
+        inside, qi, qgi = call(
+            advance_kernel,
+            [state(inner), gram(inner), grad(inner)],
+            (mix, states, weight, root_w, obs_w),
+            "vvvvv",
+            scratch(inner),
+        )
+        parts = (edges, inside)
+    return call(
+        last_kernel,
+        [state(patches)],
+        (loc, locg, msg) + parts,
+        "vvv" + "v" * len(parts),
+        (state(patches), dma((slots * patches,))),
+        out_kinds="h",
+    )[0]
 
 
 def solution(mesh):

time: 48.7 us -> 40.6 us (0.83)
  local copies, waits for them, and re-layouts: 5.04 us -> 0 us
  starting transfers between devices: 12.5 us -> 9.25 us
  Pallas kernels: 19.6 us -> 21.7 us
  waiting for transfers between devices: 11.2 us -> 9.3 us
    unnamed x12 -> x0, local copies, waits for them, and re-layouts: 5.04 us -> none
    ppermute x2, waiting for transfers between devices: 4.63 us -> 1.26 us  [neighbours(): lax.ppermute(far, 'region', cross)]
    ppermute x2, starting transfers between devices: 8.69 us -> 6.14 us  [neighbours(): lax.ppermute(far, 'region', cross)]
    pallas_call x5 -> x7, Pallas kernels: 19.6 us -> 21.7 us  [call(): pl.pallas_call(kernel, out_shape=outs, in_specs=[spec(k) for k in kinds],...]
    ppermute x2, waiting for transfers between devices: 6.56 us -> 8.04 us  [over_slots(): return lax.ppermute(msg, 'slot', [(0, 1), (1, 0)])]
    ppermute x2, starting transfers between devices: 3.8 us -> 3.1 us  [over_slots(): return lax.ppermute(msg, 'slot', [(0, 1), (1, 0)])]
  transfers between devices with their start and end apart: 6 -> 6, of which waited for: 4 -> 3; matrix products, arithmetic and copies ran while one was open for 0% -> 0% of each run, Pallas kernels for 0% -> 20%
where the time goes in v1:
time: 40.6 us; the launch traced here: 40.5 us
  Pallas kernels  21.7 us (53%)
  waiting for transfers between devices  9.3 us (23%)
  starting transfers between devices  9.25 us (23%)
    pallas_call x7, Pallas kernels, call(): pl.pallas_call(kernel, out_shape=outs, in_specs=[spec(k) for k in kinds],...  21.7 us
    ppermute x2, waiting for transfers between devices, over_slots(): return lax.ppermute(msg, 'slot', [(0, 1), (1, 0)])  8.04 us
    ppermute x2, starting transfers between devices, neighbours(): lax.ppermute(far, 'region', cross)  6.14 us
    ppermute x2, starting transfers between devices, over_slots(): return lax.ppermute(msg, 'slot', [(0, 1), (1, 0)])  3.1 us
    ppermute x2, waiting for transfers between devices, neighbours(): lax.ppermute(far, 'region', cross)  1.26 us
  transfers between devices with their start and end apart: 6, of which 3 were waited for; matrix products, arithmetic and copies ran while one was open for 0% of the time, Pallas kernels for 20%

profile of v1, /device:TPU:0, one launch (start us, length us, event | category | flops | bytes accessed | tf_op | source)
XLA Modules:
  0.0 40.5 jit_solution(2074480382419182372)
XLA Ops:
  0.0 3.2 %first_kernel.1 = (bf16[2,8,512,128]{3,2,1,0:T(8,128)(2,1)S(1)}, bf16[1024,512]{1,0:T(8,128)(2,1)S(1)}, f32[2,128,128]{2,1,0:T(8,128)S(1)}, f32[2,128]{1,0:T(2,1...) custom-call(s32[1]{0:T(128)} %bitcast.odd_ref, ...), custom_call_target="tpu_custom_call" | custom-call | flops 1000000000 | tf_op jit(solution)/shard_map/first_kernel/pallas_call | solution.py:358
  3.2 5.5 %collective-permute-start = (bf16[144,128]{1,0:T(8,128)(2,1)S(1)}, bf16[144,128]{1,0:T(8,128)(2,1)S(1)}, u32[]{:S(2)}, u32[]{:S(2)}) collective-permute-start(bf16[144,128]{1,0:T(8,128)(2,1)S(1)} %get-tuple-element.38), channel_id=1, source_target_pairs={{0,15},{1,2},{2,1},{3,4},{4,3},{5,6},{6,5},{7,8},{8,7},{9,10},{10,... | collective-permute-start | bytes 110600 | tf_op jit(solution)/shard_map/ppermute | solution.py:374
  8.8 0.0 collective-permute-start.1
  8.8 3.8 %inner_kernel.1 = (f32[6,128,128]{2,1,0:T(8,128)S(1)}, f32[6,128]{1,0:T(8,128)S(1)}) custom-call(bf16[2,8,512,128]{3,2,1,0:T(8,128)(2,1)S(1)} %get-tuple-element.32.states_ref, bf16[1024,512]{1,0:T(8,128)(2,1)S(1)} %get-tuple-element.33.w_ref, f32[2,1024,128]{2,1,0:T(8,128)S(1)} %get-tuple-element.34.rw_ref, bf16[16,2048]{1,0:T(8,128)(2,1)S(1)} %get-tuple-element.35.ow_ref), custom_call_target="tpu_custom_call" | custom-call | flops 1000000000 | tf_op jit(solution)/shard_map/inner_kernel/pallas_call | solution.py:358
  12.6 0.0 collective-permute-done.far_ref
  12.6 0.0 collective-permute-done.1.near_ref
  12.6 0.1 combine_kernel.2
  12.7 1.5 %collective-permute-start.2 = (bf16[528,128]{1,0:T(8,128)(2,1)S(1)}, bf16[528,128]{1,0:T(8,128)(2,1)S(1)}, u32[]{:S(2)}, u32[]{:S(2)}) collective-permute-start(bf16[528,128]{1,0:T(8,128)(2,1)S(1)} %get-tuple-element.42), channel_id=1, source_target_pairs={{0,16},{16,0},{1,17},{17,1},{2,18},{18,2},{3,19},{19,3},{4,20},{20... | collective-permute-start | bytes 405512 | tf_op jit(solution)/shard_map/ppermute | solution.py:380
  14.3 4.5 %collective-permute-done.2.msg_ref = bf16[528,128]{1,0:T(8,128)(2,1)S(1)} collective-permute-done((bf16[528,128]{1,0:T(8,128)(2,1)S(1)}, bf16[528,128]{1,0:T(8,128)(2,1)S(1)}, u32[]{:S(2)}, u32[]{:S(2)}) %collective-permute-start.2) | collective-permute-done | bytes 135200 | tf_op jit(solution)/shard_map/ppermute | solution.py:380
  18.8 5.1 %root_kernel.1 = (bf16[6,128,128]{2,1,0:T(8,128)(2,1)S(1)}, bf16[2,2,512,128]{3,2,1,0:T(8,128)(2,1)S(1)}, f32[2,128,128]{2,1,0:T(8,128)S(1)}, f32[2,128]{1,0:T(2...) custom-call(s32[1]{0:T(128)} %bitcast.odd_ref, f32[8,128,128]{2,1,0:T(8,128)S(1)} %get-tuple-element.40.loc_ref, ...), custom_call_target="tpu_custom_call" | custom-call | flops 1000000000 | tf_op jit(solution)/shard_map/root_kernel/pallas_call | solution.py:358
  23.9 0.6 %collective-permute-start.3 = (bf16[144,128]{1,0:T(8,128)(2,1)S(1)}, bf16[144,128]{1,0:T(8,128)(2,1)S(1)}, u32[]{:S(2)}, u32[]{:S(2)}) collective-permute-start(bf16[144,128]{1,0:T(8,128)(2,1)S(1)} %get-tuple-element.48), channel_id=1, source_target_pairs={{0,15},{1,2},{2,1},{3,4},{4,3},{5,6},{6,5},{7,8},{8,7},{9,10},{10,... | collective-permute-start | bytes 110600 | tf_op jit(solution)/shard_map/ppermute | solution.py:374
  24.5 0.0 collective-permute-start.4
  24.5 4.3 %advance_kernel.1 = (bf16[2,6,512,128]{3,2,1,0:T(8,128)(2,1)S(1)}, f32[6,128,128]{2,1,0:T(8,128)S(1)}, f32[6,128]{1,0:T(8,128)S(1)}) custom-call(bf16[6,128,128]{2,1,0:T(8,128)(2,1)S(1)} %get-tuple-element.45.mix_ref, bf16[2,8,512,128]{3,2,1,0:T(8,128)(2,1)S(1)} %get-tuple-element.32.states_ref, bf16[1024,512]{1,0:T(8,128)(2,1)S(1)} %get-tuple-element.33.w_ref, ...), custom_call_target="tpu_custom_call" | custom-call | flops 1000000000 | tf_op jit(solution)/shard_map/advance_kernel/pallas_call | solution.py:358
  28.8 1.3 %collective-permute-done.3.far_ref = bf16[144,128]{1,0:T(8,128)(2,1)S(1)} collective-permute-done((bf16[144,128]{1,0:T(8,128)(2,1)S(1)}, bf16[144,128]{1,0:T(8,128)(2,1)S(1)}, u32[]{:S(2)}, u32[]{:S(2)}) %collective-permute-start.3) | collective-permute-done | bytes 36896 | tf_op jit(solution)/shard_map/ppermute | solution.py:374
  30.0 0.0 collective-permute-done.4.near_ref
  30.0 0.1 combine_kernel.3
  30.2 1.6 %collective-permute-start.5 = (bf16[528,128]{1,0:T(8,128)(2,1)S(1)}, bf16[528,128]{1,0:T(8,128)(2,1)S(1)}, u32[]{:S(2)}, u32[]{:S(2)}) collective-permute-start(bf16[528,128]{1,0:T(8,128)(2,1)S(1)} %get-tuple-element.52), channel_id=1, source_target_pairs={{0,16},{16,0},{1,17},{17,1},{2,18},{18,2},{3,19},{19,3},{4,20},{20... | collective-permute-start | bytes 405512 | tf_op jit(solution)/shard_map/ppermute | solution.py:380
  31.7 3.5 %collective-permute-done.5.msg_ref = bf16[528,128]{1,0:T(8,128)(2,1)S(1)} collective-permute-done((bf16[528,128]{1,0:T(8,128)(2,1)S(1)}, bf16[528,128]{1,0:T(8,128)(2,1)S(1)}, u32[]{:S(2)}, u32[]{:S(2)}) %collective-permute-start.5) | collective-permute-done | bytes 135200 | tf_op jit(solution)/shard_map/ppermute | solution.py:380
  35.2 5.1 %last_kernel.1 = bf16[2,8,512,128]{3,2,1,0:T(8,128)(2,1)} custom-call(f32[8,128,128]{2,1,0:T(8,128)S(1)} %get-tuple-element.50.loc_ref, f32[8,128]{1,0:T(8,128)S(1)} %get-tuple-element.51.locg_ref, bf16[528,128]{1,0:T(8,128)(2,1)S(1)} %collective-permute-done.5.msg_ref, bf16[2,2,512,128]{3,2,1,0:T(8,128)(2,1)S(1)} %get-tuple-element.53.refs_0_, ...), custom_call_target="tpu_custom_call" | custom-call | flops 1000000000 | tf_op jit(solution)/shard_map/last_kernel/pallas_call | solution.py:358
Async XLA Ops:
  3.2 9.3 %collective-permute-start = (bf16[144,128]{1,0:T(8,128)(2,1)S(1)}, bf16[144,128]{1,0:T(8,128)(2,1)S(1)}, u32[]{:S(2)}, u32[]{:S(2)}) collective-permute-start(bf16[144,128]{1,0:T(8,128)(2,1)S(1)} %get-tuple-element.38), channel_id=1, source_target_pairs={{0,15},{1,2},{2,1},{3,4},{4,3},{5,6},{6,5},{7,8},{8,7},{9,10},{10,... | collective-permute-start | bytes 110600 | tf_op jit(solution)/shard_map/ppermute | solution.py:374
  8.8 3.8 %collective-permute-start.1 = (bf16[144,128]{1,0:T(8,128)(2,1)S(1)}, bf16[144,128]{1,0:T(8,128)(2,1)S(1)}, u32[]{:S(2)}, u32[]{:S(2)}) collective-permute-start(bf16[144,128]{1,0:T(8,128)(2,1)S(1)} %get-tuple-element.39), channel_id=1, source_target_pairs={{0,1},{1,0},{2,3},{3,2},{4,5},{5,4},{6,7},{7,6},{8,9},{9,8},{10,11... | collective-permute-start | bytes 110600 | tf_op jit(solution)/shard_map/ppermute | solution.py:374
  12.7 6.1 %collective-permute-start.2 = (bf16[528,128]{1,0:T(8,128)(2,1)S(1)}, bf16[528,128]{1,0:T(8,128)(2,1)S(1)}, u32[]{:S(2)}, u32[]{:S(2)}) collective-permute-start(bf16[528,128]{1,0:T(8,128)(2,1)S(1)} %get-tuple-element.42), channel_id=1, source_target_pairs={{0,16},{16,0},{1,17},{17,1},{2,18},{18,2},{3,19},{19,3},{4,20},{20... | collective-permute-start | bytes 405512 | tf_op jit(solution)/shard_map/ppermute | solution.py:380
  23.9 6.1 %collective-permute-start.3 = (bf16[144,128]{1,0:T(8,128)(2,1)S(1)}, bf16[144,128]{1,0:T(8,128)(2,1)S(1)}, u32[]{:S(2)}, u32[]{:S(2)}) collective-permute-start(bf16[144,128]{1,0:T(8,128)(2,1)S(1)} %get-tuple-element.48), channel_id=1, source_target_pairs={{0,15},{1,2},{2,1},{3,4},{4,3},{5,6},{6,5},{7,8},{8,7},{9,10},{10,... | collective-permute-start | bytes 110600 | tf_op jit(solution)/shard_map/ppermute | solution.py:374
  24.5 5.5 %collective-permute-start.4 = (bf16[144,128]{1,0:T(8,128)(2,1)S(1)}, bf16[144,128]{1,0:T(8,128)(2,1)S(1)}, u32[]{:S(2)}, u32[]{:S(2)}) collective-permute-start(bf16[144,128]{1,0:T(8,128)(2,1)S(1)} %get-tuple-element.49), channel_id=1, source_target_pairs={{0,1},{1,0},{2,3},{3,2},{4,5},{5,4},{6,7},{7,6},{8,9},{9,8},{10,11... | collective-permute-start | bytes 110600 | tf_op jit(solution)/shard_map/ppermute | solution.py:374
  30.2 5.1 %collective-permute-start.5 = (bf16[528,128]{1,0:T(8,128)(2,1)S(1)}, bf16[528,128]{1,0:T(8,128)(2,1)S(1)}, u32[]{:S(2)}, u32[]{:S(2)}) collective-permute-start(bf16[528,128]{1,0:T(8,128)(2,1)S(1)} %get-tuple-element.52), channel_id=1, source_target_pairs={{0,16},{16,0},{1,17},{17,1},{2,18},{18,2},{3,19},{19,3},{4,20},{20... | collective-permute-start | bytes 405512 | tf_op jit(solution)/shard_map/ppermute | solution.py:380

commit v2 on v1

--- a/solution.py
+++ b/solution.py
@@ -55,7 +55,7 @@
         ow_ref[:, t * channels : (t + 1) * channels] = rows.astype(BF16)
 
 
-def quads(items, squash, w_ref, rw_ref, ow_ref, store, sq_s, x_s):
+def quads(items, squash, w_ref, rw_ref, ow_ref, store, sq_s, x_s, before_a=None, before_b=None):
     slots, channels, members = rw_ref.shape
 
     def stage_a(i):
@@ -87,8 +87,12 @@
     n = len(items)
     for i in range(n + 2):
         if i < n:
+            if before_a is not None:
+                before_a(i)
             stage_a(i)
         if 0 <= i - 1 < n:
+            if before_b is not None:
+                before_b(i - 1)
             stage_b(i - 1)
         if 0 <= i - 2 < n:
             stage_c(i - 2)
@@ -103,18 +107,16 @@
     near_ref[...] = jnp.where(odd, low, high).astype(BF16)
 
 
-def localize(odd, edge_refs, inner_refs, far_ref, near_ref):
+def localize(odd, edge_refs, insides, far, near):
     q_edge, qg_edge = edge_refs
-    q_inner, qg_inner = inner_refs
+    q_inner, qg_inner = insides
     members = q_edge.shape[-1]
-    far = far_ref[...].astype(F32)
-    near = near_ref[...].astype(F32)
     left = jnp.where(odd, near, far)
     right = jnp.where(odd, far, near)
-    inner = q_inner.shape[0]
-    grams = [left[:members], q_edge[0]] + [q_inner[p] for p in range(inner)] + [q_edge[1], right[:members]]
+    inner = len(q_inner)
+    grams = [left[:members], q_edge[0]] + list(q_inner) + [q_edge[1], right[:members]]
     tail = slice(members, members + 1)
-    grads = [left[tail], qg_edge[0:1]] + [qg_inner[p : p + 1] for p in range(inner)] + [qg_edge[1:2], right[tail]]
+    grads = [left[tail], qg_edge[0:1]] + list(qg_inner) + [qg_edge[1:2], right[tail]]
     mix = lambda v, p: v[p + 1] + LOCAL_WEIGHT * (v[p] + v[p + 2])
     return [mix(grams, p) for p in range(inner + 2)], [mix(grads, p) for p in range(inner + 2)]
 
@@ -233,7 +235,8 @@
     return store
 
 
-def edge_quads(odd, patches, squash, w_ref, rw_ref, ow_ref, q_ref, qg_ref, far_ref, near_ref, sq_s, x_s):
+def edge_quads(odd, patches, squash, w_ref, rw_ref, ow_ref, q_ref, qg_ref, far_ref, near_ref, sq_s, x_s,
+               **hooks):
     ends = [0, patches - 1]
     found = {}
 
@@ -243,7 +246,7 @@
         q_ref[k] = gram
         qg_ref[k : k + 1] = grad
 
-    quads(ends, squash, w_ref, rw_ref, ow_ref, store, sq_s, x_s)
+    quads(ends, squash, w_ref, rw_ref, ow_ref, store, sq_s, x_s, **hooks)
     edges_of(odd, found[ends[0]], found[ends[1]], far_ref, near_ref)
 
 
@@ -266,28 +269,50 @@
         for p in range(patches)
         for t in range(slots)
     }
-    early = [state[t, p] for p in ends for t in range(slots)]
-    for c in early + [weights] + small:
+    for c in small:
         c.start()
+    for p in ends:
+        for t in range(slots):
+            state[t, p].start()
+    weights.start()
     late = [state[t, p] for p in range(1, patches - 1) for t in range(slots)]
-    for c in late:
-        c.start()
-    for c in early + [weights] + small:
-        c.wait()
-    prepare(obs_s, prec_s, mask_s, rw_ref, ow_ref)
+
+    def before_a(i):
+        for t in range(slots):
+            state[t, ends[i]].wait()
+
+    def before_b(i):
+        if i == 0:
+            for c in small:
+                c.wait()
+            prepare(obs_s, prec_s, mask_s, rw_ref, ow_ref)
+            weights.wait()
+            for c in late:
+                c.start()
+
     edge_quads(odd_ref[0] == 1, patches, squash_of(states_ref), w_ref, rw_ref, ow_ref,
-               q_ref, qg_ref, far_ref, near_ref, sq_s, x_s)
+               q_ref, qg_ref, far_ref, near_ref, sq_s, x_s, before_a=before_a, before_b=before_b)
     for c in late:
         c.wait()
 
 
-def inner_kernel(states_ref, w_ref, rw_ref, ow_ref, q_ref, qg_ref, sq_s, x_s):
+def inner_kernel(role, odd_ref, far_ref, states_ref, w_ref, rw_ref, ow_ref, q_ref, qg_ref, out_ref, sq_s, x_s):
     items = list(range(1, states_ref.shape[1] - 1))
-    quads(items, squash_of(states_ref), w_ref, rw_ref, ow_ref, into(q_ref, qg_ref, 1), sq_s, x_s)
-
-
-def combine_kernel(odd_ref, qe_ref, qge_ref, qi_ref, qgi_ref, far_ref, near_ref, loc_ref, locg_ref, msg_ref):
-    grams, grads = localize(odd_ref[0] == 1, (qe_ref, qge_ref), (qi_ref, qgi_ref), far_ref, near_ref)
+    out_ref[...] = far_ref[...]
+
+    @pl.when(odd_ref[0] == role)
+    def _():
+        quads(items, squash_of(states_ref), w_ref, rw_ref, ow_ref, into(q_ref, qg_ref, 1), sq_s, x_s)
+
+
+def combine_kernel(odd_ref, qe_ref, qge_ref, q0_ref, qg0_ref, q1_ref, qg1_ref, even_ref, odd_in_ref, near_ref,
+                   loc_ref, locg_ref, msg_ref):
+    odd = odd_ref[0] == 1
+    inner = q0_ref.shape[0]
+    q = [jnp.where(odd, q1_ref[p], q0_ref[p]) for p in range(inner)]
+    qg = [jnp.where(odd, qg1_ref[p : p + 1], qg0_ref[p : p + 1]) for p in range(inner)]
+    far = jnp.where(odd, odd_in_ref[...].astype(F32), even_ref[...].astype(F32))
+    grams, grads = localize(odd, (qe_ref, qge_ref), (q, qg), far, near_ref[...].astype(F32))
     for p in range(len(grams)):
         loc_ref[p] = grams[p]
         locg_ref[p : p + 1] = grads[p]
@@ -323,25 +348,28 @@
         self.ref[where[0], self.items.index(where[1])] = value
 
 
-def advance_kernel(mix_ref, states_ref, w_ref, rw_ref, ow_ref, new_ref, q_ref, qg_ref, sq_s, x_s):
+def advance_kernel(role, odd_ref, far_ref, mix_ref, states_ref, w_ref, rw_ref, ow_ref,
+                   new_ref, q_ref, qg_ref, out_ref, sq_s, x_s):
     items = list(range(1, states_ref.shape[1] - 1))
-    squash = advance(states_ref, lambda p: mix_ref[p - 1], _Placed(new_ref, items))
-    quads(items, squash, w_ref, rw_ref, ow_ref, into(q_ref, qg_ref, 1), sq_s, x_s)
-
-
-def last_kernel(loc_ref, locg_ref, msg_ref, *refs):
-    *states, out_hbm, out_s, sems = refs
+    out_ref[...] = far_ref[...]
+
+    @pl.when(odd_ref[0] == role)
+    def _():
+        squash = advance(states_ref, lambda p: mix_ref[p - 1], _Placed(new_ref, items))
+        quads(items, squash, w_ref, rw_ref, ow_ref, into(q_ref, qg_ref, 1), sq_s, x_s)
+
+
+def last_kernel(odd_ref, loc_ref, locg_ref, msg_ref, edges_ref, even_ref, odd_in_ref, out_hbm, out_s, sems):
     mixing = [m.astype(BF16) for m in inverse_roots(*totals(loc_ref, locg_ref, msg_ref))]
+    odd = odd_ref[0] == 1
     slots, patches = out_s.shape[:2]
     copies = []
     for p in range(patches):
         for t in range(slots):
-            if len(states) == 1:
-                value = states[0][t, p]
-            elif p in (0, patches - 1):
-                value = states[0][t, min(p, 1)]
+            if p in (0, patches - 1):
+                value = edges_ref[t, min(p, 1)]
             else:
-                value = states[1][t, p - 1]
+                value = jnp.where(odd, odd_in_ref[t, p - 1], even_ref[t, p - 1])
             out_s[t, p] = dot_nt(value, mixing[p]).astype(BF16)
             copies.append(pltpu.make_async_copy(out_s.at[t, p], out_hbm.at[t, p], sems.at[len(copies)]))
             copies[-1].start()
@@ -363,15 +391,21 @@
         scratch_shapes=[pltpu.VMEM(*s) if isinstance(s, tuple) else s for s in scratch],
         cost_estimate=pl.CostEstimate(flops=flops, bytes_accessed=0, transcendentals=0),
         compiler_params=pltpu.CompilerParams(vmem_limit_bytes=VMEM_LIMIT),
-        name=kernel.__name__,
+        name=getattr(kernel, "func", kernel).__name__,
     )(*args)
 
 
-def neighbours(far, near):
+def exchange(far, near, between):
     count = lax.axis_size("region")
     mate = [(r, r ^ 1) for r in range(count)]
-    cross = [(r, (r + 1) % count if r % 2 else (r - 1) % count) for r in range(count)]
-    return lax.ppermute(far, "region", cross), lax.ppermute(near, "region", mate)
+    up = [(r, (r + 1) % count) for r in range(1, count, 2)]
+    down = [(r, (r - 1) % count) for r in range(0, count, 2)]
+    near = lax.ppermute(near, "region", mate)
+    even_in = lax.ppermute(far, "region", up)
+    *first, far = between(0, far)
+    odd_in = lax.ppermute(far, "region", down)
+    *second, _ = between(1, far)
+    return first, second, (even_in, odd_in, near)
 
 
 def over_slots(msg):
@@ -417,23 +451,28 @@
             dma((4 + slots * patches,)),
         ),
     )
-    far, near = neighbours(far, near)
-    qi, qgi = call(
-        inner_kernel, [gram(inner), grad(inner)], (states, weight, root_w, obs_w), "vvvv", scratch(inner)
-    )
-    parts = (states,)
+    def plain(role, far):
+        return call(
+            functools.partial(inner_kernel, role),
+            [gram(inner), grad(inner), edge],
+            (odd, far, states, weight, root_w, obs_w),
+            "svvvvv",
+            scratch(inner),
+        )
+
+    first, second, received = exchange(far, near, plain)
     for step in range(OUTER):
         loc, locg, msg = call(
             combine_kernel,
             [gram(patches), grad(patches), msg_shape],
-            (odd, qe, qge, qi, qgi, far, near),
-            "svvvvvv",
+            (odd, qe, qge, *first[-2:], *second[-2:], *received),
+            "s" + "v" * 9,
         )
         msg = over_slots(msg)
         if step == OUTER - 1:
             break
-        if len(parts) > 1:
-            edges, inside = parts
+        if step:
+            inside = jnp.where(odd == 1, second[0], first[0])
             states = jnp.concatenate([edges[:, :1], inside, edges[:, 1:]], axis=1)
         mix, edges, qe, qge, far, near = call(
             root_kernel,
@@ -442,20 +481,22 @@
             "svvvvvvv",
             scratch(2),
         )
-        far, near = neighbours(far, near)
-        inside, qi, qgi = call(
-            advance_kernel,
-            [state(inner), gram(inner), grad(inner)],
-            (mix, states, weight, root_w, obs_w),
-            "vvvvv",
-            scratch(inner),
-        )
-        parts = (edges, inside)
+
+        def moving(role, far):
+            return call(
+                functools.partial(advance_kernel, role),
+                [state(inner), gram(inner), grad(inner), edge],
+                (odd, far, mix, states, weight, root_w, obs_w),
+                "svvvvvv",
+                scratch(inner),
+            )
+
+        first, second, received = exchange(far, near, moving)
     return call(
         last_kernel,
         [state(patches)],
-        (loc, locg, msg) + parts,
-        "vvv" + "v" * len(parts),
+        (odd, loc, locg, msg, edges, first[0], second[0]),
+        "svvvvvv",
         (state(patches), dma((slots * patches,))),
         out_kinds="h",
     )[0]

time: 40.6 us -> 46.9 us (1.16)
  starting transfers between devices: 9.25 us -> 13.5 us
  Pallas kernels: 21.7 us -> 24.1 us
  waiting for transfers between devices: 9.3 us -> 8.77 us
    ppermute x4 -> x6, starting transfers between devices: 6.14 us -> 9.93 us  [the longest x2 6.73 us: exchange(): odd_in = lax.ppermute(far, 'region', down)]
    pallas_call x7 -> x9, Pallas kernels: 21.7 us -> 24.1 us  [call(): pl.pallas_call(kernel, out_shape=outs, in_specs=[spec(k) for k in kinds],...]
    ppermute x2, waiting for transfers between devices: 8.04 us -> 7.19 us  [over_slots(): return lax.ppermute(msg, 'slot', [(0, 1), (1, 0)])]
    ppermute x4 -> x6, waiting for transfers between devices: 1.26 us -> 1.57 us  [the longest x2 1.56 us: exchange(): odd_in = lax.ppermute(far, 'region', down)]
  transfers between devices with their start and end apart: 6 -> 8, of which waited for: 3 -> 4; matrix products, arithmetic and copies ran while one was open for 0% -> 0% of each run, Pallas kernels for 20% -> 20%
where the time goes in v2:
time: 46.9 us; the launch traced here: 46.6 us
  Pallas kernels  24.1 us (51%)
  starting transfers between devices  13.5 us (29%)
  waiting for transfers between devices  8.77 us (19%)
    pallas_call x9, Pallas kernels, call(): pl.pallas_call(kernel, out_shape=outs, in_specs=[spec(k) for k in kinds],...  24.1 us
    ppermute x2, waiting for transfers between devices, over_slots(): return lax.ppermute(msg, 'slot', [(0, 1), (1, 0)])  7.19 us
    ppermute x2, starting transfers between devices, exchange(): odd_in = lax.ppermute(far, 'region', down)  6.73 us
    ppermute x2, starting transfers between devices, over_slots(): return lax.ppermute(msg, 'slot', [(0, 1), (1, 0)])  3.54 us
    ppermute x2, starting transfers between devices, exchange(): even_in = lax.ppermute(far, 'region', up)  2.57 us
    ppermute x2, waiting for transfers between devices, exchange(): odd_in = lax.ppermute(far, 'region', down)  1.56 us
  transfers between devices with their start and end apart: 8, of which 4 were waited for; matrix products, arithmetic and copies ran while one was open for 0% of the time, Pallas kernels for 20%

profile of v2, /device:TPU:0, one launch (start us, length us, event | category | flops | bytes accessed | tf_op | source)
XLA Modules:
  0.0 46.6 jit_solution(10756947708771837307)
XLA Ops:
  0.0 4.2 %first_kernel.1 = (bf16[2,8,512,128]{3,2,1,0:T(8,128)(2,1)S(1)}, bf16[1024,512]{1,0:T(8,128)(2,1)S(1)}, f32[2,128,128]{2,1,0:T(8,128)S(1)}, f32[2,128]{1,0:T(2,1...) custom-call(s32[1]{0:T(128)} %bitcast.odd_ref, ...), custom_call_target="tpu_custom_call" | custom-call | flops 1000000000 | tf_op jit(solution)/shard_map/first_kernel/pallas_call | solution.py:386
  4.2 0.6 %collective-permute-start.2 = (bf16[144,128]{1,0:T(8,128)(2,1)S(1)}, bf16[144,128]{1,0:T(8,128)(2,1)S(1)}, u32[]{:S(2)}, u32[]{:S(2)}) collective-permute-start(bf16[144,128]{1,0:T(8,128)(2,1)S(1)} %get-tuple-element.49), channel_id=1, source_target_pairs={{0,1},{1,0},{2,3},{3,2},{4,5},{5,4},{6,7},{7,6},{8,9},{9,8},{10,11... | collective-permute-start | bytes 110600 | tf_op jit(solution)/shard_map/ppermute | solution.py:403
  4.8 1.3 %collective-permute-start = (bf16[144,128]{1,0:T(8,128)(2,1)S(1)}, bf16[144,128]{1,0:T(8,128)(2,1)S(1)}, u32[]{:S(2)}, u32[]{:S(2)}) collective-permute-start(bf16[144,128]{1,0:T(8,128)(2,1)S(1)} %get-tuple-element.39.far_ref), channel_id=1, source_target_pairs={{1,2},{3,4},{5,6},{7,8},{9,10},{11,12},{13,14},{15,0},{17,18},{19,... | collective-permute-start | bytes 110600 | tf_op jit(solution)/shard_map/ppermute | solution.py:404
  6.1 3.7 %inner_kernel.2 = (f32[6,128,128]{2,1,0:T(8,128)S(1)}, f32[6,128]{1,0:T(8,128)S(1)}, bf16[144,128]{1,0:T(8,128)(2,1)S(1)}) custom-call(s32[1]{0:T(128)} %bitcast.odd_ref, bf16[144,128]{1,0:T(8,128)(2,1)S(1)} %get-tuple-element.39.far_ref, bf16[2,8,512,128]{3,2,1,0:T(8,128)(2,1)S(1)} %get-tuple-element.40.states_ref, ...), custom_call_target="tpu_custom_call" | custom-call | flops 1000000000 | tf_op jit(solution)/shard_map/inner_kernel/pallas_call | solution.py:386
  9.8 3.8 %collective-permute-start.1 = (bf16[144,128]{1,0:T(8,128)(2,1)S(1)}, bf16[144,128]{1,0:T(8,128)(2,1)S(1)}, u32[]{:S(2)}, u32[]{:S(2)}) collective-permute-start(bf16[144,128]{1,0:T(8,128)(2,1)S(1)} %get-tuple-element.46.far_ref), channel_id=1, source_target_pairs={{0,15},{2,1},{4,3},{6,5},{8,7},{10,9},{12,11},{14,13},{16,31},{18,... | collective-permute-start | bytes 110600 | tf_op jit(solution)/shard_map/ppermute | solution.py:406
  13.7 0.8 %inner_kernel.3 = (f32[6,128,128]{2,1,0:T(8,128)S(1)}, f32[6,128]{1,0:T(8,128)S(1)}, bf16[144,128]{1,0:T(8,128)(2,1)}) custom-call(s32[1]{0:T(128)} %bitcast.odd_ref, bf16[144,128]{1,0:T(8,128)(2,1)S(1)} %get-tuple-element.46.far_ref, bf16[2,8,512,128]{3,2,1,0:T(8,128)(2,1)S(1)} %get-tuple-element.40.states_ref, ...), custom_call_target="tpu_custom_call" | custom-call | flops 1000000000 | tf_op jit(solution)/shard_map/inner_kernel/pallas_call | solution.py:386
  14.5 0.0 collective-permute-done.2.near_ref
  14.5 0.0 collective-permute-done.even_ref
  14.5 0.8 %collective-permute-done.1.odd_in_ref = bf16[144,128]{1,0:T(8,128)(2,1)S(1)} collective-permute-done((bf16[144,128]{1,0:T(8,128)(2,1)S(1)}, bf16[144,128]{1,0:T(8,128)(2,1)S(1)}, u32[]{:S(2)}, u32[]{:S(2)}) %collective-permute-start.1) | collective-permute-done | bytes 36896 | tf_op jit(solution)/shard_map/ppermute | solution.py:406
  15.3 0.2 combine_kernel.2
  15.5 2.0 %collective-permute-start.3 = (bf16[528,128]{1,0:T(8,128)(2,1)S(1)}, bf16[528,128]{1,0:T(8,128)(2,1)S(1)}, u32[]{:S(2)}, u32[]{:S(2)}) collective-permute-start(bf16[528,128]{1,0:T(8,128)(2,1)S(1)} %get-tuple-element.52), channel_id=1, source_target_pairs={{0,16},{16,0},{1,17},{17,1},{2,18},{18,2},{3,19},{19,3},{4,20},{20... | collective-permute-start | bytes 405512 | tf_op jit(solution)/shard_map/ppermute | solution.py:414
  17.4 3.7 %collective-permute-done.3.msg_ref = bf16[528,128]{1,0:T(8,128)(2,1)S(1)} collective-permute-done((bf16[528,128]{1,0:T(8,128)(2,1)S(1)}, bf16[528,128]{1,0:T(8,128)(2,1)S(1)}, u32[]{:S(2)}, u32[]{:S(2)}) %collective-permute-start.3) | collective-permute-done | bytes 135200 | tf_op jit(solution)/shard_map/ppermute | solution.py:414
  21.1 5.1 %root_kernel.1 = (bf16[6,128,128]{2,1,0:T(8,128)(2,1)S(1)}, bf16[2,2,512,128]{3,2,1,0:T(8,128)(2,1)S(1)}, f32[2,128,128]{2,1,0:T(8,128)S(1)}, f32[2,128]{1,0:T(2...) custom-call(s32[1]{0:T(128)} %bitcast.odd_ref, f32[8,128,128]{2,1,0:T(8,128)S(1)} %get-tuple-element.50.loc_ref, ...), custom_call_target="tpu_custom_call" | custom-call | flops 1000000000 | tf_op jit(solution)/shard_map/root_kernel/pallas_call | solution.py:386
  26.2 0.1 collective-permute-start.6
  26.3 1.3 %collective-permute-start.4 = (bf16[144,128]{1,0:T(8,128)(2,1)S(1)}, bf16[144,128]{1,0:T(8,128)(2,1)S(1)}, u32[]{:S(2)}, u32[]{:S(2)}) collective-permute-start(bf16[144,128]{1,0:T(8,128)(2,1)S(1)} %get-tuple-element.55.far_ref), channel_id=1, source_target_pairs={{1,2},{3,4},{5,6},{7,8},{9,10},{11,12},{13,14},{15,0},{17,18},{19,... | collective-permute-start | bytes 110600 | tf_op jit(solution)/shard_map/ppermute | solution.py:404
  27.6 4.1 %advance_kernel.2 = (bf16[2,6,512,128]{3,2,1,0:T(8,128)(2,1)S(1)}, f32[6,128,128]{2,1,0:T(8,128)S(1)}, f32[6,128]{1,0:T(8,128)S(1)}, bf16[144,128]{1,0:T(8,128)(2,1)S(1)}) custom-call(s32[1]{0:T(128)} %bitcast.odd_ref, bf16[144,128]{1,0:T(8,128)(2,1)S(1)} %get-tuple-element.55.far_ref, bf16[6,128,128]{2,1,0:T(8,128)(2,1)S(1)} %get-tuple-element.56.mix_ref, ...), custom_call_target="tpu_custom_call" | custom-call | flops 1000000000 | tf_op jit(solution)/shard_map/advance_kernel/pallas_call | solution.py:386
  31.6 2.9 %collective-permute-start.5 = (bf16[144,128]{1,0:T(8,128)(2,1)S(1)}, bf16[144,128]{1,0:T(8,128)(2,1)S(1)}, u32[]{:S(2)}, u32[]{:S(2)}) collective-permute-start(bf16[144,128]{1,0:T(8,128)(2,1)S(1)} %get-tuple-element.59.far_ref), channel_id=1, source_target_pairs={{0,15},{2,1},{4,3},{6,5},{8,7},{10,9},{12,11},{14,13},{16,31},{18,... | collective-permute-start | bytes 110600 | tf_op jit(solution)/shard_map/ppermute | solution.py:406
  34.6 0.8 %advance_kernel.3 = (bf16[2,6,512,128]{3,2,1,0:T(8,128)(2,1)S(1)}, f32[6,128,128]{2,1,0:T(8,128)S(1)}, f32[6,128]{1,0:T(8,128)S(1)}, bf16[144,128]{1,0:T(8,128)(2,1)}) custom-call(s32[1]{0:T(128)} %bitcast.odd_ref, bf16[144,128]{1,0:T(8,128)(2,1)S(1)} %get-tuple-element.59.far_ref, bf16[6,128,128]{2,1,0:T(8,128)(2,1)S(1)} %get-tuple-element.56.mix_ref, ...), custom_call_target="tpu_custom_call" | custom-call | flops 1000000000 | tf_op jit(solution)/shard_map/advance_kernel/pallas_call | solution.py:386
  35.4 0.0 collective-permute-done.4.even_ref
  35.4 0.8 %collective-permute-done.5.odd_in_ref = bf16[144,128]{1,0:T(8,128)(2,1)S(1)} collective-permute-done((bf16[144,128]{1,0:T(8,128)(2,1)S(1)}, bf16[144,128]{1,0:T(8,128)(2,1)S(1)}, u32[]{:S(2)}, u32[]{:S(2)}) %collective-permute-start.5) | collective-permute-done | bytes 36896 | tf_op jit(solution)/shard_map/ppermute | solution.py:406
  36.2 0.2 combine_kernel.3
  36.3 1.6 %collective-permute-start.7 = (bf16[528,128]{1,0:T(8,128)(2,1)S(1)}, bf16[528,128]{1,0:T(8,128)(2,1)S(1)}, u32[]{:S(2)}, u32[]{:S(2)}) collective-permute-start(bf16[528,128]{1,0:T(8,128)(2,1)S(1)} %get-tuple-element.65), channel_id=1, source_target_pairs={{0,16},{16,0},{1,17},{17,1},{2,18},{18,2},{3,19},{19,3},{4,20},{20... | collective-permute-start | bytes 405512 | tf_op jit(solution)/shard_map/ppermute | solution.py:414
  37.9 3.5 %collective-permute-done.7.msg_ref = bf16[528,128]{1,0:T(8,128)(2,1)S(1)} collective-permute-done((bf16[528,128]{1,0:T(8,128)(2,1)S(1)}, bf16[528,128]{1,0:T(8,128)(2,1)S(1)}, u32[]{:S(2)}, u32[]{:S(2)}) %collective-permute-start.7) | collective-permute-done | bytes 135200 | tf_op jit(solution)/shard_map/ppermute | solution.py:414
  41.4 5.1 %last_kernel.1 = bf16[2,8,512,128]{3,2,1,0:T(8,128)(2,1)} custom-call(s32[1]{0:T(128)} %bitcast.odd_ref, f32[8,128,128]{2,1,0:T(8,128)S(1)} %get-tuple-element.63.loc_ref, f32[8,128]{1,0:T(8,128)S(1)} %get-tuple-element.64.locg_ref, bf16[528,128]{1,0:T(8,128)(2,1)S(1)} %collective-permute-done.7.msg_ref, ...), custom_call_target="tpu_custom_call" | custom-call | flops 1000000000 | tf_op jit(solution)/shard_map/last_kernel/pallas_call | solution.py:386
  (1 shorter events, 0.0 us)
Async XLA Ops:
  4.2 10.2 %collective-permute-start.2 = (bf16[144,128]{1,0:T(8,128)(2,1)S(1)}, bf16[144,128]{1,0:T(8,128)(2,1)S(1)}, u32[]{:S(2)}, u32[]{:S(2)}) collective-permute-start(bf16[144,128]{1,0:T(8,128)(2,1)S(1)} %get-tuple-element.49), channel_id=1, source_target_pairs={{0,1},{1,0},{2,3},{3,2},{4,5},{5,4},{6,7},{7,6},{8,9},{9,8},{10,11... | collective-permute-start | bytes 110600 | tf_op jit(solution)/shard_map/ppermute | solution.py:403
  4.8 9.7 %collective-permute-start = (bf16[144,128]{1,0:T(8,128)(2,1)S(1)}, bf16[144,128]{1,0:T(8,128)(2,1)S(1)}, u32[]{:S(2)}, u32[]{:S(2)}) collective-permute-start(bf16[144,128]{1,0:T(8,128)(2,1)S(1)} %get-tuple-element.39.far_ref), channel_id=1, source_target_pairs={{1,2},{3,4},{5,6},{7,8},{9,10},{11,12},{13,14},{15,0},{17,18},{19,... | collective-permute-start | bytes 110600 | tf_op jit(solution)/shard_map/ppermute | solution.py:404
  9.8 5.5 %collective-permute-start.1 = (bf16[144,128]{1,0:T(8,128)(2,1)S(1)}, bf16[144,128]{1,0:T(8,128)(2,1)S(1)}, u32[]{:S(2)}, u32[]{:S(2)}) collective-permute-start(bf16[144,128]{1,0:T(8,128)(2,1)S(1)} %get-tuple-element.46.far_ref), channel_id=1, source_target_pairs={{0,15},{2,1},{4,3},{6,5},{8,7},{10,9},{12,11},{14,13},{16,31},{18,... | collective-permute-start | bytes 110600 | tf_op jit(solution)/shard_map/ppermute | solution.py:406
  15.5 5.7 %collective-permute-start.3 = (bf16[528,128]{1,0:T(8,128)(2,1)S(1)}, bf16[528,128]{1,0:T(8,128)(2,1)S(1)}, u32[]{:S(2)}, u32[]{:S(2)}) collective-permute-start(bf16[528,128]{1,0:T(8,128)(2,1)S(1)} %get-tuple-element.52), channel_id=1, source_target_pairs={{0,16},{16,0},{1,17},{17,1},{2,18},{18,2},{3,19},{19,3},{4,20},{20... | collective-permute-start | bytes 405512 | tf_op jit(solution)/shard_map/ppermute | solution.py:414
  26.2 9.2 %collective-permute-start.6 = (bf16[144,128]{1,0:T(8,128)(2,1)S(1)}, bf16[144,128]{1,0:T(8,128)(2,1)S(1)}, u32[]{:S(2)}, u32[]{:S(2)}) collective-permute-start(bf16[144,128]{1,0:T(8,128)(2,1)S(1)} %get-tuple-element.62), channel_id=1, source_target_pairs={{0,1},{1,0},{2,3},{3,2},{4,5},{5,4},{6,7},{7,6},{8,9},{9,8},{10,11... | collective-permute-start | bytes 110600 | tf_op jit(solution)/shard_map/ppermute | solution.py:403
  26.3 9.1 %collective-permute-start.4 = (bf16[144,128]{1,0:T(8,128)(2,1)S(1)}, bf16[144,128]{1,0:T(8,128)(2,1)S(1)}, u32[]{:S(2)}, u32[]{:S(2)}) collective-permute-start(bf16[144,128]{1,0:T(8,128)(2,1)S(1)} %get-tuple-element.55.far_ref), channel_id=1, source_target_pairs={{1,2},{3,4},{5,6},{7,8},{9,10},{11,12},{13,14},{15,0},{17,18},{19,... | collective-permute-start | bytes 110600 | tf_op jit(solution)/shard_map/ppermute | solution.py:404
  31.6 4.5 %collective-permute-start.5 = (bf16[144,128]{1,0:T(8,128)(2,1)S(1)}, bf16[144,128]{1,0:T(8,128)(2,1)S(1)}, u32[]{:S(2)}, u32[]{:S(2)}) collective-permute-start(bf16[144,128]{1,0:T(8,128)(2,1)S(1)} %get-tuple-element.59.far_ref), channel_id=1, source_target_pairs={{0,15},{2,1},{4,3},{6,5},{8,7},{10,9},{12,11},{14,13},{16,31},{18,... | collective-permute-start | bytes 110600 | tf_op jit(solution)/shard_map/ppermute | solution.py:406
  36.3 5.1 %collective-permute-start.7 = (bf16[528,128]{1,0:T(8,128)(2,1)S(1)}, bf16[528,128]{1,0:T(8,128)(2,1)S(1)}, u32[]{:S(2)}, u32[]{:S(2)}) collective-permute-start(bf16[528,128]{1,0:T(8,128)(2,1)S(1)} %get-tuple-element.65), channel_id=1, source_target_pairs={{0,16},{16,0},{1,17},{17,1},{2,18},{18,2},{3,19},{19,3},{4,20},{20... | collective-permute-start | bytes 405512 | tf_op jit(solution)/shard_map/ppermute | solution.py:414

commit v3 on v1

--- a/solution.py
+++ b/solution.py
@@ -23,11 +23,6 @@
 
 def dot_nt(a, b):
     return lax.dot_general(a, b, (((1,), (1,)), ((), ())), preferred_element_type=F32)
-
-
-def split(x):
-    hi = x.astype(BF16)
-    return hi, (x - hi.astype(F32)).astype(BF16)
 
 
 def cat(parts, axis):
@@ -55,7 +50,7 @@
         ow_ref[:, t * channels : (t + 1) * channels] = rows.astype(BF16)
 
 
-def quads(items, squash, w_ref, rw_ref, ow_ref, store, sq_s, x_s):
+def quads(items, squash, w_ref, rw_ref, ow_ref, store, sq_s, x_s, before_a=None, before_b=None):
     slots, channels, members = rw_ref.shape
 
     def stage_a(i):
@@ -85,13 +80,17 @@
         store(items[i], square - row - (col - total), grad)
 
     n = len(items)
-    for i in range(n + 2):
+    for i in range(n + 1):
         if i < n:
+            if before_a is not None:
+                before_a(i)
             stage_a(i)
-        if 0 <= i - 1 < n:
+        if i:
+            if before_b is not None:
+                before_b(i - 1)
             stage_b(i - 1)
-        if 0 <= i - 2 < n:
-            stage_c(i - 2)
+    for i in range(n):
+        stage_c(i)
 
 
 def edges_of(odd, low, high, far_ref, near_ref):
@@ -151,64 +150,67 @@
 
 def inverse_roots(grams, grads):
     members = grams[0].shape[0]
-    n = len(grams)
-    every = range(n)
+    every = range(len(grams))
     rid, cid = iotas(members)
     identity = jnp.where(rid == cid, 1.0, 0.0).astype(F32)
-    zero = jnp.zeros((members, members), BF16)
     shifted = [g + (members - 1.0) * identity for g in grams]
     square = [jnp.sum(jnp.sum(s * s, axis=0, keepdims=True), axis=1, keepdims=True) for s in shifted]
     norm = [jnp.sqrt(s) for s in square]
     t = [shifted[i] * (1.0 / norm[i]) for i in every]
-    z = [None] * n
+    y = [jnp.broadcast_to(g, (8, members)) for g in grads]
+
+    def with_row(mat, row):
+        high = row.astype(BF16).astype(F32)
+        return cat([mat, cat([high, row - high], 0).astype(BF16)], 0)
+
+    def row_of(prod):
+        return prod[members : members + 8, :members] + prod[members + 8 :, :members]
+
+    def in_pairs(left, right):
+        out = []
+        for i in range(0, len(left), 2):
+            zero = jnp.zeros_like(right[i])
+            both = cat([cat([right[i], zero], 1), cat([zero, right[i + 1]], 1)], 0)
+            prod = dot(cat(left[i : i + 2], 1), both)
+            out += [prod[:, :members], prod[:, members:]]
+        return out
+
+    z = [None for _ in every]
     for step in range(NS_SPLIT):
-        sp = [split(v) for v in t]
+        th = [v.astype(BF16) for v in t]
         if step == 0:
-            prod = [
-                dot(cat([h, l], 1), cat([cat([h, l], 1), cat([h, zero], 1)], 0)) for h, l in sp
-            ]
-            sq = [v[:, :members] + v[:, members:] for v in prod]
+            prod = [dot(with_row(th[i], y[i]), th[i]) for i in every]
             z = [1.5 * identity - 0.5 * v for v in t]
         else:
-            zs = [split(v) for v in z]
-            prod = []
-            for (h, l), (zh, zl) in zip(sp, zs):
-                top = cat([h, zh], 1)
-                prod.append(dot(cat([h, l], 1), cat([top, top], 0)) + dot(h, cat([l, zl], 1)))
-            sq = [v[:, :members] for v in prod]
-            z = [1.5 * z[i] - 0.5 * prod[i][:, members:] for i in every]
-        x = [split(1.5 * t[i] - 0.25 * sq[i]) for i in every]
-        prod = [
-            dot(cat([x[i][0], x[i][1]], 1), cat([cat(sp[i], 1), cat([sp[i][0], zero], 1)], 0))
-            for i in every
-        ]
-        t = [2.25 * t[i] - (prod[i][:, :members] + prod[i][:, members:]) for i in every]
+            prod = [dot(with_row(th[i], y[i]), cat([th[i], z[i].astype(BF16)], 1)) for i in every]
+            z = [1.5 * z[i] - 0.5 * prod[i][:members, members:] for i in every]
+        y = [1.5 * y[i] - 0.5 * row_of(prod[i]) for i in every]
+        x = [(1.5 * t[i] - 0.25 * prod[i][:members, :members]).astype(BF16) for i in every]
+        shrunk = in_pairs(x, th)
+        t = [2.25 * t[i] - shrunk[i] for i in every]
     d = [identity - v for v in t]
     for step in range(NS_SPLIT, NS_STEPS):
         dh = [v.astype(BF16) for v in d]
+        prod = [dot(with_row(dh[i], y[i]), cat([dh[i], z[i].astype(BF16)], 1)) for i in every]
+        z = [z[i] + 0.5 * prod[i][:members, members:] for i in every]
+        y = [y[i] + 0.5 * row_of(prod[i]) for i in every]
         if step < NS_STEPS - 1:
-            prod = [dot(dh[i], cat([dh[i], z[i].astype(BF16)], 1)) for i in every]
-            z = [z[i] + 0.5 * prod[i][:, members:] for i in every]
-            d2 = [v[:, :members] for v in prod]
-            d = [0.75 * d2[i] + 0.25 * dot(d2[i].astype(BF16), dh[i]) for i in every]
-        else:
-            z = [z[i] + 0.5 * dot(dh[i], z[i].astype(BF16)) for i in every]
-
-    def rowdot(v, zs):
-        h, l = split(jnp.broadcast_to(v, (8, members)))
-        both = dot(cat([h, l], 1), cat([cat(zs, 1), cat([zs[0], zero], 1)], 0))
-        return (both[:, :members] + both[:, members:])[0:1]
-
-    zs = [split(v) for v in z]
-    inner = [rowdot(grads[i], zs[i]) for i in every]
-    along = [rowdot(inner[i], zs[i]) / norm[i] for i in every]
+            d2 = [v[:members, :members] for v in prod]
+            d3 = in_pairs([v.astype(BF16) for v in d2], dh)
+            d = [0.75 * d2[i] + 0.25 * d3[i] for i in every]
+
     scale = math.sqrt(members - 1.0)
+    share = 1.0 / members
     out = []
     for i in every:
-        root = z[i] * (scale / jnp.sqrt(norm[i]))
-        col = jnp.sum(root, axis=1, keepdims=True) * (1.0 / members)
-        shift = along[i] - jnp.sum(along[i], axis=1, keepdims=True) * (1.0 / members) + 1.0 / members
-        out.append((root - col) + shift)
+        yn = y[i] * (1.0 / norm[i])
+        high = yn.astype(BF16).astype(F32)
+        rows = dot(cat([high, yn - high], 0).astype(BF16), z[i].astype(BF16))
+        along = (rows[:8] + rows[8:])[0:1]
+        row = jnp.sum(z[i], axis=0, keepdims=True) * share
+        col = jnp.sum(z[i], axis=1, keepdims=True) * share
+        level = jnp.sum(yn[0:1] * row, axis=1, keepdims=True)
+        out.append((z[i] - col) * (scale / jnp.sqrt(norm[i])) + (along - level + share))
     return out
 
 
@@ -233,7 +235,8 @@
     return store
 
 
-def edge_quads(odd, patches, squash, w_ref, rw_ref, ow_ref, q_ref, qg_ref, far_ref, near_ref, sq_s, x_s):
+def edge_quads(odd, patches, squash, w_ref, rw_ref, ow_ref, q_ref, qg_ref, far_ref, near_ref, sq_s, x_s,
+               **hooks):
     ends = [0, patches - 1]
     found = {}
 
@@ -243,7 +246,7 @@
         q_ref[k] = gram
         qg_ref[k : k + 1] = grad
 
-    quads(ends, squash, w_ref, rw_ref, ow_ref, store, sq_s, x_s)
+    quads(ends, squash, w_ref, rw_ref, ow_ref, store, sq_s, x_s, **hooks)
     edges_of(odd, found[ends[0]], found[ends[1]], far_ref, near_ref)
 
 
@@ -266,17 +269,29 @@
         for p in range(patches)
         for t in range(slots)
     }
-    early = [state[t, p] for p in ends for t in range(slots)]
-    for c in early + [weights] + small:
+    for c in small:
         c.start()
+    for p in ends:
+        for t in range(slots):
+            state[t, p].start()
+    weights.start()
     late = [state[t, p] for p in range(1, patches - 1) for t in range(slots)]
     for c in late:
         c.start()
-    for c in early + [weights] + small:
-        c.wait()
-    prepare(obs_s, prec_s, mask_s, rw_ref, ow_ref)
+
+    def before_a(i):
+        for t in range(slots):
+            state[t, ends[i]].wait()
+
+    def before_b(i):
+        if i == 0:
+            for c in small:
+                c.wait()
+            prepare(obs_s, prec_s, mask_s, rw_ref, ow_ref)
+            weights.wait()
+
     edge_quads(odd_ref[0] == 1, patches, squash_of(states_ref), w_ref, rw_ref, ow_ref,
-               q_ref, qg_ref, far_ref, near_ref, sq_s, x_s)
+               q_ref, qg_ref, far_ref, near_ref, sq_s, x_s, before_a=before_a, before_b=before_b)
     for c in late:
         c.wait()
 

time: 40.6 us -> 39.2 us (0.966)
  Pallas kernels: 21.7 us -> 19.9 us
    pallas_call x7, Pallas kernels: 21.7 us -> 19.9 us  [call(): pl.pallas_call(kernel, out_shape=outs, in_specs=[spec(k) for k in kinds],...]
    ppermute x2, waiting for transfers between devices: 1.26 us -> 1.68 us  [neighbours(): lax.ppermute(far, 'region', cross)]
  transfers between devices with their start and end apart: 6 -> 6, of which waited for: 3 -> 3; matrix products, arithmetic and copies ran while one was open for 0% -> 0% of each run, Pallas kernels for 20% -> 18%
where the time goes in v3:
time: 39.2 us; the launch traced here: 39.1 us
  Pallas kernels  19.9 us (51%)
  waiting for transfers between devices  9.7 us (25%)
  starting transfers between devices  9.32 us (24%)
    pallas_call x7, Pallas kernels, call(): pl.pallas_call(kernel, out_shape=outs, in_specs=[spec(k) for k in kinds],...  19.9 us
    ppermute x2, waiting for transfers between devices, over_slots(): return lax.ppermute(msg, 'slot', [(0, 1), (1, 0)])  8.01 us
    ppermute x2, starting transfers between devices, neighbours(): lax.ppermute(far, 'region', cross)  6.19 us
    ppermute x2, starting transfers between devices, over_slots(): return lax.ppermute(msg, 'slot', [(0, 1), (1, 0)])  3.13 us
    ppermute x2, waiting for transfers between devices, neighbours(): lax.ppermute(far, 'region', cross)  1.68 us
  transfers between devices with their start and end apart: 6, of which 3 were waited for; matrix products, arithmetic and copies ran while one was open for 0% of the time, Pallas kernels for 18%

profile of v3, /device:TPU:0, one launch (start us, length us, event | category | flops | bytes accessed | tf_op | source)
XLA Modules:
  0.0 39.1 jit_solution(11525290402232674283)
XLA Ops:
  0.0 3.1 %first_kernel.1 = (bf16[2,8,512,128]{3,2,1,0:T(8,128)(2,1)S(1)}, bf16[1024,512]{1,0:T(8,128)(2,1)S(1)}, f32[2,128,128]{2,1,0:T(8,128)S(1)}, f32[2,128]{1,0:T(2,1...) custom-call(s32[1]{0:T(128)} %bitcast.odd_ref, ...), custom_call_target="tpu_custom_call" | custom-call | flops 1000000000 | tf_op jit(solution)/shard_map/first_kernel/pallas_call | solution.py:373
  3.2 5.5 %collective-permute-start = (bf16[144,128]{1,0:T(8,128)(2,1)S(1)}, bf16[144,128]{1,0:T(8,128)(2,1)S(1)}, u32[]{:S(2)}, u32[]{:S(2)}) collective-permute-start(bf16[144,128]{1,0:T(8,128)(2,1)S(1)} %get-tuple-element.38), channel_id=1, source_target_pairs={{0,15},{1,2},{2,1},{3,4},{4,3},{5,6},{6,5},{7,8},{8,7},{9,10},{10,... | collective-permute-start | bytes 110600 | tf_op jit(solution)/shard_map/ppermute | solution.py:389
  8.7 0.0 collective-permute-start.1
  8.7 3.3 %inner_kernel.1 = (f32[6,128,128]{2,1,0:T(8,128)S(1)}, f32[6,128]{1,0:T(8,128)S(1)}) custom-call(bf16[2,8,512,128]{3,2,1,0:T(8,128)(2,1)S(1)} %get-tuple-element.32.states_ref, bf16[1024,512]{1,0:T(8,128)(2,1)S(1)} %get-tuple-element.33.w_ref, f32[2,1024,128]{2,1,0:T(8,128)S(1)} %get-tuple-element.34.rw_ref, bf16[16,2048]{1,0:T(8,128)(2,1)S(1)} %get-tuple-element.35.ow_ref), custom_call_target="tpu_custom_call" | custom-call | flops 1000000000 | tf_op jit(solution)/shard_map/inner_kernel/pallas_call | solution.py:373
  12.0 0.0 collective-permute-done.far_ref
  12.0 0.0 collective-permute-done.1.near_ref
  12.0 0.1 combine_kernel.2
  12.2 1.6 %collective-permute-start.2 = (bf16[528,128]{1,0:T(8,128)(2,1)S(1)}, bf16[528,128]{1,0:T(8,128)(2,1)S(1)}, u32[]{:S(2)}, u32[]{:S(2)}) collective-permute-start(bf16[528,128]{1,0:T(8,128)(2,1)S(1)} %get-tuple-element.42), channel_id=1, source_target_pairs={{0,16},{16,0},{1,17},{17,1},{2,18},{18,2},{3,19},{19,3},{4,20},{20... | collective-permute-start | bytes 405512 | tf_op jit(solution)/shard_map/ppermute | solution.py:395
  13.7 4.5 %collective-permute-done.2.msg_ref = bf16[528,128]{1,0:T(8,128)(2,1)S(1)} collective-permute-done((bf16[528,128]{1,0:T(8,128)(2,1)S(1)}, bf16[528,128]{1,0:T(8,128)(2,1)S(1)}, u32[]{:S(2)}, u32[]{:S(2)}) %collective-permute-start.2) | collective-permute-done | bytes 135200 | tf_op jit(solution)/shard_map/ppermute | solution.py:395
  18.2 4.5 %root_kernel.1 = (bf16[6,128,128]{2,1,0:T(8,128)(2,1)S(1)}, bf16[2,2,512,128]{3,2,1,0:T(8,128)(2,1)S(1)}, f32[2,128,128]{2,1,0:T(8,128)S(1)}, f32[2,128]{1,0:T(2...) custom-call(s32[1]{0:T(128)} %bitcast.odd_ref, f32[8,128,128]{2,1,0:T(8,128)S(1)} %get-tuple-element.40.loc_ref, ...), custom_call_target="tpu_custom_call" | custom-call | flops 1000000000 | tf_op jit(solution)/shard_map/root_kernel/pallas_call | solution.py:373
  22.8 0.7 %collective-permute-start.3 = (bf16[144,128]{1,0:T(8,128)(2,1)S(1)}, bf16[144,128]{1,0:T(8,128)(2,1)S(1)}, u32[]{:S(2)}, u32[]{:S(2)}) collective-permute-start(bf16[144,128]{1,0:T(8,128)(2,1)S(1)} %get-tuple-element.48), channel_id=1, source_target_pairs={{0,15},{1,2},{2,1},{3,4},{4,3},{5,6},{6,5},{7,8},{8,7},{9,10},{10,... | collective-permute-start | bytes 110600 | tf_op jit(solution)/shard_map/ppermute | solution.py:389
  23.4 0.0 collective-permute-start.4
  23.4 3.8 %advance_kernel.1 = (bf16[2,6,512,128]{3,2,1,0:T(8,128)(2,1)S(1)}, f32[6,128,128]{2,1,0:T(8,128)S(1)}, f32[6,128]{1,0:T(8,128)S(1)}) custom-call(bf16[6,128,128]{2,1,0:T(8,128)(2,1)S(1)} %get-tuple-element.45.mix_ref, bf16[2,8,512,128]{3,2,1,0:T(8,128)(2,1)S(1)} %get-tuple-element.32.states_ref, bf16[1024,512]{1,0:T(8,128)(2,1)S(1)} %get-tuple-element.33.w_ref, ...), custom_call_target="tpu_custom_call" | custom-call | flops 1000000000 | tf_op jit(solution)/shard_map/advance_kernel/pallas_call | solution.py:373
  27.2 1.7 %collective-permute-done.3.far_ref = bf16[144,128]{1,0:T(8,128)(2,1)S(1)} collective-permute-done((bf16[144,128]{1,0:T(8,128)(2,1)S(1)}, bf16[144,128]{1,0:T(8,128)(2,1)S(1)}, u32[]{:S(2)}, u32[]{:S(2)}) %collective-permute-start.3) | collective-permute-done | bytes 36896 | tf_op jit(solution)/shard_map/ppermute | solution.py:389
  28.9 0.0 collective-permute-done.4.near_ref
  28.9 0.1 combine_kernel.3
  29.1 1.6 %collective-permute-start.5 = (bf16[528,128]{1,0:T(8,128)(2,1)S(1)}, bf16[528,128]{1,0:T(8,128)(2,1)S(1)}, u32[]{:S(2)}, u32[]{:S(2)}) collective-permute-start(bf16[528,128]{1,0:T(8,128)(2,1)S(1)} %get-tuple-element.52), channel_id=1, source_target_pairs={{0,16},{16,0},{1,17},{17,1},{2,18},{18,2},{3,19},{19,3},{4,20},{20... | collective-permute-start | bytes 405512 | tf_op jit(solution)/shard_map/ppermute | solution.py:395
  30.6 3.5 %collective-permute-done.5.msg_ref = bf16[528,128]{1,0:T(8,128)(2,1)S(1)} collective-permute-done((bf16[528,128]{1,0:T(8,128)(2,1)S(1)}, bf16[528,128]{1,0:T(8,128)(2,1)S(1)}, u32[]{:S(2)}, u32[]{:S(2)}) %collective-permute-start.5) | collective-permute-done | bytes 135200 | tf_op jit(solution)/shard_map/ppermute | solution.py:395
  34.1 4.8 %last_kernel.1 = bf16[2,8,512,128]{3,2,1,0:T(8,128)(2,1)} custom-call(f32[8,128,128]{2,1,0:T(8,128)S(1)} %get-tuple-element.50.loc_ref, f32[8,128]{1,0:T(8,128)S(1)} %get-tuple-element.51.locg_ref, bf16[528,128]{1,0:T(8,128)(2,1)S(1)} %collective-permute-done.5.msg_ref, bf16[2,2,512,128]{3,2,1,0:T(8,128)(2,1)S(1)} %get-tuple-element.53.refs_0_, ...), custom_call_target="tpu_custom_call" | custom-call | flops 1000000000 | tf_op jit(solution)/shard_map/last_kernel/pallas_call | solution.py:373
Async XLA Ops:
  3.2 8.9 %collective-permute-start = (bf16[144,128]{1,0:T(8,128)(2,1)S(1)}, bf16[144,128]{1,0:T(8,128)(2,1)S(1)}, u32[]{:S(2)}, u32[]{:S(2)}) collective-permute-start(bf16[144,128]{1,0:T(8,128)(2,1)S(1)} %get-tuple-element.38), channel_id=1, source_target_pairs={{0,15},{1,2},{2,1},{3,4},{4,3},{5,6},{6,5},{7,8},{8,7},{9,10},{10,... | collective-permute-start | bytes 110600 | tf_op jit(solution)/shard_map/ppermute | solution.py:389
  8.7 3.3 %collective-permute-start.1 = (bf16[144,128]{1,0:T(8,128)(2,1)S(1)}, bf16[144,128]{1,0:T(8,128)(2,1)S(1)}, u32[]{:S(2)}, u32[]{:S(2)}) collective-permute-start(bf16[144,128]{1,0:T(8,128)(2,1)S(1)} %get-tuple-element.39), channel_id=1, source_target_pairs={{0,1},{1,0},{2,3},{3,2},{4,5},{5,4},{6,7},{7,6},{8,9},{9,8},{10,11... | collective-permute-start | bytes 110600 | tf_op jit(solution)/shard_map/ppermute | solution.py:389
  12.2 6.1 %collective-permute-start.2 = (bf16[528,128]{1,0:T(8,128)(2,1)S(1)}, bf16[528,128]{1,0:T(8,128)(2,1)S(1)}, u32[]{:S(2)}, u32[]{:S(2)}) collective-permute-start(bf16[528,128]{1,0:T(8,128)(2,1)S(1)} %get-tuple-element.42), channel_id=1, source_target_pairs={{0,16},{16,0},{1,17},{17,1},{2,18},{18,2},{3,19},{19,3},{4,20},{20... | collective-permute-start | bytes 405512 | tf_op jit(solution)/shard_map/ppermute | solution.py:395
  22.8 6.1 %collective-permute-start.3 = (bf16[144,128]{1,0:T(8,128)(2,1)S(1)}, bf16[144,128]{1,0:T(8,128)(2,1)S(1)}, u32[]{:S(2)}, u32[]{:S(2)}) collective-permute-start(bf16[144,128]{1,0:T(8,128)(2,1)S(1)} %get-tuple-element.48), channel_id=1, source_target_pairs={{0,15},{1,2},{2,1},{3,4},{4,3},{5,6},{6,5},{7,8},{8,7},{9,10},{10,... | collective-permute-start | bytes 110600 | tf_op jit(solution)/shard_map/ppermute | solution.py:389
  23.4 5.5 %collective-permute-start.4 = (bf16[144,128]{1,0:T(8,128)(2,1)S(1)}, bf16[144,128]{1,0:T(8,128)(2,1)S(1)}, u32[]{:S(2)}, u32[]{:S(2)}) collective-permute-start(bf16[144,128]{1,0:T(8,128)(2,1)S(1)} %get-tuple-element.49), channel_id=1, source_target_pairs={{0,1},{1,0},{2,3},{3,2},{4,5},{5,4},{6,7},{7,6},{8,9},{9,8},{10,11... | collective-permute-start | bytes 110600 | tf_op jit(solution)/shard_map/ppermute | solution.py:389
  29.1 5.1 %collective-permute-start.5 = (bf16[528,128]{1,0:T(8,128)(2,1)S(1)}, bf16[528,128]{1,0:T(8,128)(2,1)S(1)}, u32[]{:S(2)}, u32[]{:S(2)}) collective-permute-start(bf16[528,128]{1,0:T(8,128)(2,1)S(1)} %get-tuple-element.52), channel_id=1, source_target_pairs={{0,16},{16,0},{1,17},{17,1},{2,18},{18,2},{3,19},{19,3},{4,20},{20... | collective-permute-start | bytes 405512 | tf_op jit(solution)/shard_map/ppermute | solution.py:395

commit v4 on v3

--- a/solution.py
+++ b/solution.py
@@ -102,20 +102,8 @@
     near_ref[...] = jnp.where(odd, low, high).astype(BF16)
 
 
-def localize(odd, edge_refs, inner_refs, far_ref, near_ref):
-    q_edge, qg_edge = edge_refs
-    q_inner, qg_inner = inner_refs
-    members = q_edge.shape[-1]
-    far = far_ref[...].astype(F32)
-    near = near_ref[...].astype(F32)
-    left = jnp.where(odd, near, far)
-    right = jnp.where(odd, far, near)
-    inner = q_inner.shape[0]
-    grams = [left[:members], q_edge[0]] + [q_inner[p] for p in range(inner)] + [q_edge[1], right[:members]]
-    tail = slice(members, members + 1)
-    grads = [left[tail], qg_edge[0:1]] + [qg_inner[p : p + 1] for p in range(inner)] + [qg_edge[1:2], right[tail]]
-    mix = lambda v, p: v[p + 1] + LOCAL_WEIGHT * (v[p] + v[p + 2])
-    return [mix(grams, p) for p in range(inner + 2)], [mix(grads, p) for p in range(inner + 2)]
+def mixed(v):
+    return [v[p + 1] + LOCAL_WEIGHT * (v[p] + v[p + 2]) for p in range(len(v) - 2)]
 
 
 def pack(grams, grads, out_ref):
@@ -156,7 +144,7 @@
     shifted = [g + (members - 1.0) * identity for g in grams]
     square = [jnp.sum(jnp.sum(s * s, axis=0, keepdims=True), axis=1, keepdims=True) for s in shifted]
     norm = [jnp.sqrt(s) for s in square]
-    t = [shifted[i] * (1.0 / norm[i]) for i in every]
+    inv = [1.0 / v for v in norm]
     y = [jnp.broadcast_to(g, (8, members)) for g in grads]
 
     def with_row(mat, row):
@@ -177,16 +165,22 @@
 
     z = [None for _ in every]
     for step in range(NS_SPLIT):
-        th = [v.astype(BF16) for v in t]
         if step == 0:
-            prod = [dot(with_row(th[i], y[i]), th[i]) for i in every]
+            th = [v.astype(BF16) for v in shifted]
+            prod = [dot(with_row(th[i], y[i]), th[i]) * inv[i] for i in every]
+            t = [shifted[i] * inv[i] for i in every]
+            square = [prod[i][:members] * inv[i] for i in every]
             z = [1.5 * identity - 0.5 * v for v in t]
         else:
+            th = [v.astype(BF16) for v in t]
             prod = [dot(with_row(th[i], y[i]), cat([th[i], z[i].astype(BF16)], 1)) for i in every]
+            square = [v[:members, :members] for v in prod]
             z = [1.5 * z[i] - 0.5 * prod[i][:members, members:] for i in every]
         y = [1.5 * y[i] - 0.5 * row_of(prod[i]) for i in every]
-        x = [(1.5 * t[i] - 0.25 * prod[i][:members, :members]).astype(BF16) for i in every]
+        x = [(1.5 * t[i] - 0.25 * square[i]).astype(BF16) for i in every]
         shrunk = in_pairs(x, th)
+        if step == 0:
+            shrunk = [shrunk[i] * inv[i] for i in every]
         t = [2.25 * t[i] - shrunk[i] for i in every]
     d = [identity - v for v in t]
     for step in range(NS_SPLIT, NS_STEPS):
@@ -276,12 +270,13 @@
             state[t, p].start()
     weights.start()
     late = [state[t, p] for p in range(1, patches - 1) for t in range(slots)]
-    for c in late:
-        c.start()
 
     def before_a(i):
         for t in range(slots):
             state[t, ends[i]].wait()
+        if i == 0:
+            for c in late:
+                c.start()
 
     def before_b(i):
         if i == 0:
@@ -296,32 +291,70 @@
         c.wait()
 
 
-def inner_kernel(states_ref, w_ref, rw_ref, ow_ref, q_ref, qg_ref, sq_s, x_s):
-    items = list(range(1, states_ref.shape[1] - 1))
-    quads(items, squash_of(states_ref), w_ref, rw_ref, ow_ref, into(q_ref, qg_ref, 1), sq_s, x_s)
-
-
-def combine_kernel(odd_ref, qe_ref, qge_ref, qi_ref, qgi_ref, far_ref, near_ref, loc_ref, locg_ref, msg_ref):
-    grams, grads = localize(odd_ref[0] == 1, (qe_ref, qge_ref), (qi_ref, qgi_ref), far_ref, near_ref)
-    for p in range(len(grams)):
+def finish_inner(qe_ref, qge_ref, found, outs):
+    loc_ref, locg_ref, msg_ref, q_ref, qg_ref = outs
+    inner = len(found)
+    grams = mixed([qe_ref[0]] + [found[p][0][...] for p in range(inner)] + [qe_ref[1]])
+    grads = mixed([qge_ref[0:1]] + [found[p][1] for p in range(inner)] + [qge_ref[1:2]])
+    for p in range(inner):
         loc_ref[p] = grams[p]
         locg_ref[p : p + 1] = grads[p]
     pack(grams, grads, msg_ref)
-
-
-def totals(loc_ref, locg_ref, msg_ref):
-    patches = loc_ref.shape[0]
-    grams, grads = unpack(msg_ref, patches)
-    return (
-        [loc_ref[p] + grams[p] for p in range(patches)],
-        [locg_ref[p : p + 1] + grads[p] for p in range(patches)],
-    )
-
-
-def root_kernel(odd_ref, loc_ref, locg_ref, msg_ref, states_ref, w_ref, rw_ref, ow_ref,
-                mix_ref, new_ref, q_ref, qg_ref, far_ref, near_ref, sq_s, x_s):
-    mixing = [m.astype(BF16) for m in inverse_roots(*totals(loc_ref, locg_ref, msg_ref))]
-    patches = loc_ref.shape[0]
+    for k, p in enumerate((0, inner - 1)):
+        q_ref[k] = found[p][0][...]
+        qg_ref[k : k + 1] = found[p][1]
+
+
+def inner_quads(items, squash, w_ref, rw_ref, ow_ref, qe_ref, qge_ref, outs, sq_s, x_s, q_s):
+    found = []
+
+    def store(p, gram, grad):
+        q_s[len(found)] = gram
+        found.append((q_s.at[len(found)], grad))
+
+    quads(items, squash, w_ref, rw_ref, ow_ref, store, sq_s, x_s)
+    finish_inner(qe_ref, qge_ref, found, outs)
+
+
+def inner_kernel(states_ref, w_ref, rw_ref, ow_ref, qe_ref, qge_ref, *refs):
+    *outs, sq_s, x_s, q_s = refs
+    items = list(range(1, states_ref.shape[1] - 1))
+    inner_quads(items, squash_of(states_ref), w_ref, rw_ref, ow_ref, qe_ref, qge_ref, outs, sq_s, x_s, q_s)
+
+
+def combine_kernel(odd_ref, qe_ref, qge_ref, qi_ref, qgi_ref, far_ref, near_ref, loc_ref, locg_ref, msg_ref):
+    odd = odd_ref[0] == 1
+    members = qe_ref.shape[-1]
+    far = far_ref[...].astype(F32)
+    near = near_ref[...].astype(F32)
+    left = jnp.where(odd, near, far)
+    right = jnp.where(odd, far, near)
+    tail = slice(members, members + 1)
+    grams = mixed([left[:members], qe_ref[0], qi_ref[0]]) + mixed([qi_ref[1], qe_ref[1], right[:members]])
+    grads = mixed([left[tail], qge_ref[0:1], qgi_ref[0:1]]) + mixed([qgi_ref[1:2], qge_ref[1:2], right[tail]])
+    for k in range(2):
+        loc_ref[k] = grams[k]
+        locg_ref[k : k + 1] = grads[k]
+    pack(grams, grads, msg_ref)
+
+
+def totals(refs):
+    parts = []
+    for loc_ref, locg_ref, msg_ref in (refs[:3], refs[3:]):
+        n = loc_ref.shape[0]
+        grams, grads = unpack(msg_ref, n)
+        parts.append(([loc_ref[p] + grams[p] for p in range(n)], [locg_ref[p : p + 1] + grads[p] for p in range(n)]))
+    (gi, vi), (ge, ve) = parts
+    return ge[:1] + gi + ge[1:], ve[:1] + vi + ve[1:]
+
+
+def root_kernel(odd_ref, *refs):
+    sums, (states_ref, w_ref, rw_ref, ow_ref, mix_ref, new_ref, q_ref, qg_ref, far_ref, near_ref, sq_s, x_s) = (
+        refs[:6],
+        refs[6:],
+    )
+    mixing = [m.astype(BF16) for m in inverse_roots(*totals(sums))]
+    patches = states_ref.shape[1]
     for p in range(1, patches - 1):
         mix_ref[p - 1] = mixing[p]
     ends = [0, patches - 1]
@@ -338,15 +371,16 @@
         self.ref[where[0], self.items.index(where[1])] = value
 
 
-def advance_kernel(mix_ref, states_ref, w_ref, rw_ref, ow_ref, new_ref, q_ref, qg_ref, sq_s, x_s):
+def advance_kernel(mix_ref, states_ref, w_ref, rw_ref, ow_ref, qe_ref, qge_ref, new_ref, *refs):
+    *outs, sq_s, x_s, q_s = refs
     items = list(range(1, states_ref.shape[1] - 1))
     squash = advance(states_ref, lambda p: mix_ref[p - 1], _Placed(new_ref, items))
-    quads(items, squash, w_ref, rw_ref, ow_ref, into(q_ref, qg_ref, 1), sq_s, x_s)
-
-
-def last_kernel(loc_ref, locg_ref, msg_ref, *refs):
-    *states, out_hbm, out_s, sems = refs
-    mixing = [m.astype(BF16) for m in inverse_roots(*totals(loc_ref, locg_ref, msg_ref))]
+    inner_quads(items, squash, w_ref, rw_ref, ow_ref, qe_ref, qge_ref, outs, sq_s, x_s, q_s)
+
+
+def last_kernel(*refs):
+    *states, out_hbm, out_s, sems = refs[6:]
+    mixing = [m.astype(BF16) for m in inverse_roots(*totals(refs[:6]))]
     slots, patches = out_s.shape[:2]
     copies = []
     for p in range(patches):
@@ -407,8 +441,13 @@
     edge = ((members + 16, members), BF16)
     gram = lambda n: ((n, members, members), F32)
     grad = lambda n: ((n, members), F32)
-    extra = -(-(patches // 2 + patches) // 16) * 16
-    msg_shape = ((patches // 2 * members + extra, members), BF16)
+    message = lambda n: ((n // 2 * members + -(-(n // 2 + n) // 16) * 16, members), BF16)
+    inner_out = [gram(inner), grad(inner), message(inner), gram(2), grad(2)]
+    inner_scratch = (
+        ((inner, rows, slots * members), BF16),
+        ((inner, slots * channels, members), BF16),
+        gram(inner),
+    )
     scratch = lambda n: (
         ((n, rows, slots * members), BF16),
         ((n, slots * channels, members), BF16),
@@ -433,18 +472,19 @@
         ),
     )
     far, near = neighbours(far, near)
-    qi, qgi = call(
-        inner_kernel, [gram(inner), grad(inner)], (states, weight, root_w, obs_w), "vvvv", scratch(inner)
+    *loc, msg, qi, qgi = call(
+        inner_kernel, inner_out, (states, weight, root_w, obs_w, qe, qge), "vvvvvv", inner_scratch
     )
     parts = (states,)
     for step in range(OUTER):
-        loc, locg, msg = call(
+        sums = (*loc, over_slots(msg))
+        *loc, msg = call(
             combine_kernel,
-            [gram(patches), grad(patches), msg_shape],
+            [gram(2), grad(2), message(2)],
             (odd, qe, qge, qi, qgi, far, near),
             "svvvvvv",
         )
-        msg = over_slots(msg)
+        sums += (*loc, over_slots(msg))
         if step == OUTER - 1:
             break
         if len(parts) > 1:
@@ -453,24 +493,24 @@
         mix, edges, qe, qge, far, near = call(
             root_kernel,
             [((inner, members, members), BF16), state(2), gram(2), grad(2), edge, edge],
-            (odd, loc, locg, msg, states, weight, root_w, obs_w),
-            "svvvvvvv",
+            (odd, *sums, states, weight, root_w, obs_w),
+            "s" + "v" * 10,
             scratch(2),
         )
         far, near = neighbours(far, near)
-        inside, qi, qgi = call(
+        inside, *loc, msg, qi, qgi = call(
             advance_kernel,
-            [state(inner), gram(inner), grad(inner)],
-            (mix, states, weight, root_w, obs_w),
-            "vvvvv",
-            scratch(inner),
+            [state(inner)] + inner_out,
+            (mix, states, weight, root_w, obs_w, qe, qge),
+            "vvvvvvv",
+            inner_scratch,
         )
         parts = (edges, inside)
     return call(
         last_kernel,
         [state(patches)],
-        (loc, locg, msg) + parts,
-        "vvv" + "v" * len(parts),
+        sums + parts,
+        "v" * (6 + len(parts)),
         (state(patches), dma((slots * patches,))),
         out_kinds="h",
     )[0]

time: 39.2 us -> 37.9 us (0.967)
  waiting for transfers between devices: 9.7 us -> 6.91 us
  starting transfers between devices: 9.32 us -> 11 us
    ppermute x2 -> x4, starting transfers between devices: 3.13 us -> 5.28 us  [over_slots(): return lax.ppermute(msg, 'slot', [(0, 1), (1, 0)])]
    ppermute x2 -> x4, waiting for transfers between devices: 8.01 us -> 6.41 us  [over_slots(): return lax.ppermute(msg, 'slot', [(0, 1), (1, 0)])]
    ppermute x2, waiting for transfers between devices: 1.68 us -> 0.49 us  [neighbours(): lax.ppermute(far, 'region', cross)]
    ppermute x2, starting transfers between devices: 6.19 us -> 5.74 us  [neighbours(): lax.ppermute(far, 'region', cross)]
  transfers between devices with their start and end apart: 6 -> 8, of which waited for: 3 -> 3; matrix products, arithmetic and copies ran while one was open for 0% -> 0% of each run, Pallas kernels for 18% -> 20%
where the time goes in v4:
time: 37.9 us; the launch traced here: 37.8 us
  Pallas kernels  19.6 us (52%)
  starting transfers between devices  11 us (29%)
  waiting for transfers between devices  6.91 us (18%)
    pallas_call x7, Pallas kernels, call(): pl.pallas_call(kernel, out_shape=outs, in_specs=[spec(k) for k in kinds],...  19.6 us
    ppermute x4, waiting for transfers between devices, over_slots(): return lax.ppermute(msg, 'slot', [(0, 1), (1, 0)])  6.41 us
    ppermute x2, starting transfers between devices, neighbours(): lax.ppermute(far, 'region', cross)  5.74 us
    ppermute x4, starting transfers between devices, over_slots(): return lax.ppermute(msg, 'slot', [(0, 1), (1, 0)])  5.28 us
  transfers between devices with their start and end apart: 8, of which 3 were waited for; matrix products, arithmetic and copies ran while one was open for 0% of the time, Pallas kernels for 20%

profile of v4, /device:TPU:0, one launch (start us, length us, event | category | flops | bytes accessed | tf_op | source)
XLA Modules:
  0.0 37.8 jit_solution(9481490489720485469)
XLA Ops:
  0.0 3.1 %first_kernel.1 = (bf16[2,8,512,128]{3,2,1,0:T(8,128)(2,1)S(1)}, bf16[1024,512]{1,0:T(8,128)(2,1)S(1)}, f32[2,128,128]{2,1,0:T(8,128)S(1)}, f32[2,128]{1,0:T(2,1...) custom-call(s32[1]{0:T(128)} %bitcast.odd_ref, ...), custom_call_target="tpu_custom_call" | custom-call | flops 1000000000 | tf_op jit(solution)/shard_map/first_kernel/pallas_call | solution.py:407
  3.2 5.5 %collective-permute-start.1 = (bf16[144,128]{1,0:T(8,128)(2,1)S(1)}, bf16[144,128]{1,0:T(8,128)(2,1)S(1)}, u32[]{:S(2)}, u32[]{:S(2)}) collective-permute-start(bf16[144,128]{1,0:T(8,128)(2,1)S(1)} %get-tuple-element.47), channel_id=1, source_target_pairs={{0,15},{1,2},{2,1},{3,4},{4,3},{5,6},{6,5},{7,8},{8,7},{9,10},{10,... | collective-permute-start | bytes 110600 | tf_op jit(solution)/shard_map/ppermute | solution.py:423
  8.7 0.0 collective-permute-start.2
  8.7 3.4 %inner_kernel.1 = (f32[6,128,128]{2,1,0:T(8,128)S(1)}, f32[6,128]{1,0:T(8,128)S(1)}, bf16[400,128]{1,0:T(8,128)(2,1)S(1)}, f32[2,128,128]{2,1,0:T(8,128)S(1)}, f32[2,128]{1,0:T(2,128)S(1)}) custom-call(bf16[2,8,512,128]{3,2,1,0:T(8,128)(2,1)S(1)} %get-tuple-element.36.states_ref.refs_6_, bf16[1024,512]{1,0:T(8,128)(2,1)S(1)} %get-tuple-element.37.w_ref.refs_7_, ...), custom_call_target="tpu_custom_call" | custom-call | flops 1000000000 | tf_op jit(solution)/shard_map/inner_kernel/pallas_call | solution.py:407
  12.1 1.6 %collective-permute-start = (bf16[400,128]{1,0:T(8,128)(2,1)S(1)}, bf16[400,128]{1,0:T(8,128)(2,1)S(1)}, u32[]{:S(2)}, u32[]{:S(2)}) collective-permute-start(bf16[400,128]{1,0:T(8,128)(2,1)S(1)} %get-tuple-element.44), channel_id=1, source_target_pairs={{0,16},{16,0},{1,17},{17,1},{2,18},{18,2},{3,19},{19,3},{4,20},{20... | collective-permute-start | bytes 307208 | tf_op jit(solution)/shard_map/ppermute | solution.py:429
  13.7 0.0 collective-permute-done.1.far_ref
  13.7 0.0 collective-permute-done.2.near_ref
  13.7 0.1 combine_kernel.2
  13.7 0.6 %collective-permute-start.3 = (bf16[144,128]{1,0:T(8,128)(2,1)S(1)}, bf16[144,128]{1,0:T(8,128)(2,1)S(1)}, u32[]{:S(2)}, u32[]{:S(2)}) collective-permute-start(bf16[144,128]{1,0:T(8,128)(2,1)S(1)} %get-tuple-element.51), channel_id=1, source_target_pairs={{0,16},{16,0},{1,17},{17,1},{2,18},{18,2},{3,19},{19,3},{4,20},{20... | collective-permute-start | bytes 110600 | tf_op jit(solution)/shard_map/ppermute | solution.py:429
  14.3 3.9 %collective-permute-done.3.refs_5_ = bf16[144,128]{1,0:T(8,128)(2,1)S(1)} collective-permute-done((bf16[144,128]{1,0:T(8,128)(2,1)S(1)}, bf16[144,128]{1,0:T(8,128)(2,1)S(1)}, u32[]{:S(2)}, u32[]{:S(2)}) %collective-permute-start.3) | collective-permute-done | bytes 36896 | tf_op jit(solution)/shard_map/ppermute | solution.py:429
  18.2 0.0 collective-permute-done.refs_2_
  18.2 4.4 %root_kernel.1 = (bf16[6,128,128]{2,1,0:T(8,128)(2,1)S(1)}, bf16[2,2,512,128]{3,2,1,0:T(8,128)(2,1)S(1)}, f32[2,128,128]{2,1,0:T(8,128)S(1)}, f32[2,128]{1,0:T(2...) custom-call(s32[1]{0:T(128)} %bitcast.odd_ref, f32[6,128,128]{2,1,0:T(8,128)S(1)} %get-tuple-element.42.refs_0_, ...), custom_call_target="tpu_custom_call" | custom-call | flops 1000000000 | tf_op jit(solution)/shard_map/root_kernel/pallas_call | solution.py:407
  22.7 0.2 collective-permute-start.5
  22.9 0.0 collective-permute-start.6
  22.9 3.9 %advance_kernel.1 = (bf16[2,6,512,128]{3,2,1,0:T(8,128)(2,1)S(1)}, f32[6,128,128]{2,1,0:T(8,128)S(1)}, f32[6,128]{1,0:T(8,128)S(1)}, bf16[400,128]{1,0:T(8,128)(...) custom-call(bf16[6,128,128]{2,1,0:T(8,128)(2,1)S(1)} %get-tuple-element.52.mix_ref, ...), custom_call_target="tpu_custom_call" | custom-call | flops 1000000000 | tf_op jit(solution)/shard_map/advance_kernel/pallas_call | solution.py:407
  26.8 1.6 %collective-permute-start.4 = (bf16[400,128]{1,0:T(8,128)(2,1)S(1)}, bf16[400,128]{1,0:T(8,128)(2,1)S(1)}, u32[]{:S(2)}, u32[]{:S(2)}) collective-permute-start(bf16[400,128]{1,0:T(8,128)(2,1)S(1)} %get-tuple-element.57), channel_id=1, source_target_pairs={{0,16},{16,0},{1,17},{17,1},{2,18},{18,2},{3,19},{19,3},{4,20},{20... | collective-permute-start | bytes 307208 | tf_op jit(solution)/shard_map/ppermute | solution.py:429
  28.3 0.5 %collective-permute-done.5.far_ref = bf16[144,128]{1,0:T(8,128)(2,1)S(1)} collective-permute-done((bf16[144,128]{1,0:T(8,128)(2,1)S(1)}, bf16[144,128]{1,0:T(8,128)(2,1)S(1)}, u32[]{:S(2)}, u32[]{:S(2)}) %collective-permute-start.5) | collective-permute-done | bytes 36896 | tf_op jit(solution)/shard_map/ppermute | solution.py:423
  28.8 0.0 collective-permute-done.6.near_ref
  28.8 0.1 combine_kernel.3
  28.9 1.6 %collective-permute-start.7 = (bf16[144,128]{1,0:T(8,128)(2,1)S(1)}, bf16[144,128]{1,0:T(8,128)(2,1)S(1)}, u32[]{:S(2)}, u32[]{:S(2)}) collective-permute-start(bf16[144,128]{1,0:T(8,128)(2,1)S(1)} %get-tuple-element.64), channel_id=1, source_target_pairs={{0,16},{16,0},{1,17},{17,1},{2,18},{18,2},{3,19},{19,3},{4,20},{20... | collective-permute-start | bytes 110600 | tf_op jit(solution)/shard_map/ppermute | solution.py:429
  30.5 2.5 %collective-permute-done.7.refs_5_ = bf16[144,128]{1,0:T(8,128)(2,1)S(1)} collective-permute-done((bf16[144,128]{1,0:T(8,128)(2,1)S(1)}, bf16[144,128]{1,0:T(8,128)(2,1)S(1)}, u32[]{:S(2)}, u32[]{:S(2)}) %collective-permute-start.7) | collective-permute-done | bytes 36896 | tf_op jit(solution)/shard_map/ppermute | solution.py:429
  32.9 0.0 collective-permute-done.4.refs_2_
  32.9 4.7 %last_kernel.1 = bf16[2,8,512,128]{3,2,1,0:T(8,128)(2,1)} custom-call(f32[6,128,128]{2,1,0:T(8,128)S(1)} %get-tuple-element.55.refs_0_, f32[6,128]{1,0:T(8,128)S(1)} %get-tuple-element.56.refs_1_, bf16[400,128]{1,0:T(8,128)(2,1)S(1)} %collective-permute-done.4.refs_2_, f32[2,128,128]{2,1,0:T(8,128)S(1)} %get-tuple-element.62.refs_3_, ...), custom_call_target="tpu_custom_call" | custom-call | flops 1000000000 | tf_op jit(solution)/shard_map/last_kernel/pallas_call | solution.py:407
Async XLA Ops:
  3.2 10.5 %collective-permute-start.1 = (bf16[144,128]{1,0:T(8,128)(2,1)S(1)}, bf16[144,128]{1,0:T(8,128)(2,1)S(1)}, u32[]{:S(2)}, u32[]{:S(2)}) collective-permute-start(bf16[144,128]{1,0:T(8,128)(2,1)S(1)} %get-tuple-element.47), channel_id=1, source_target_pairs={{0,15},{1,2},{2,1},{3,4},{4,3},{5,6},{6,5},{7,8},{8,7},{9,10},{10,... | collective-permute-start | bytes 110600 | tf_op jit(solution)/shard_map/ppermute | solution.py:423
  8.7 5.0 %collective-permute-start.2 = (bf16[144,128]{1,0:T(8,128)(2,1)S(1)}, bf16[144,128]{1,0:T(8,128)(2,1)S(1)}, u32[]{:S(2)}, u32[]{:S(2)}) collective-permute-start(bf16[144,128]{1,0:T(8,128)(2,1)S(1)} %get-tuple-element.48), channel_id=1, source_target_pairs={{0,1},{1,0},{2,3},{3,2},{4,5},{5,4},{6,7},{7,6},{8,9},{9,8},{10,11... | collective-permute-start | bytes 110600 | tf_op jit(solution)/shard_map/ppermute | solution.py:423
  12.1 6.2 %collective-permute-start = (bf16[400,128]{1,0:T(8,128)(2,1)S(1)}, bf16[400,128]{1,0:T(8,128)(2,1)S(1)}, u32[]{:S(2)}, u32[]{:S(2)}) collective-permute-start(bf16[400,128]{1,0:T(8,128)(2,1)S(1)} %get-tuple-element.44), channel_id=1, source_target_pairs={{0,16},{16,0},{1,17},{17,1},{2,18},{18,2},{3,19},{19,3},{4,20},{20... | collective-permute-start | bytes 307208 | tf_op jit(solution)/shard_map/ppermute | solution.py:429
  13.7 4.5 %collective-permute-start.3 = (bf16[144,128]{1,0:T(8,128)(2,1)S(1)}, bf16[144,128]{1,0:T(8,128)(2,1)S(1)}, u32[]{:S(2)}, u32[]{:S(2)}) collective-permute-start(bf16[144,128]{1,0:T(8,128)(2,1)S(1)} %get-tuple-element.51), channel_id=1, source_target_pairs={{0,16},{16,0},{1,17},{17,1},{2,18},{18,2},{3,19},{19,3},{4,20},{20... | collective-permute-start | bytes 110600 | tf_op jit(solution)/shard_map/ppermute | solution.py:429
  22.7 6.1 %collective-permute-start.5 = (bf16[144,128]{1,0:T(8,128)(2,1)S(1)}, bf16[144,128]{1,0:T(8,128)(2,1)S(1)}, u32[]{:S(2)}, u32[]{:S(2)}) collective-permute-start(bf16[144,128]{1,0:T(8,128)(2,1)S(1)} %get-tuple-element.60), channel_id=1, source_target_pairs={{0,15},{1,2},{2,1},{3,4},{4,3},{5,6},{6,5},{7,8},{8,7},{9,10},{10,... | collective-permute-start | bytes 110600 | tf_op jit(solution)/shard_map/ppermute | solution.py:423
  22.9 5.9 %collective-permute-start.6 = (bf16[144,128]{1,0:T(8,128)(2,1)S(1)}, bf16[144,128]{1,0:T(8,128)(2,1)S(1)}, u32[]{:S(2)}, u32[]{:S(2)}) collective-permute-start(bf16[144,128]{1,0:T(8,128)(2,1)S(1)} %get-tuple-element.61), channel_id=1, source_target_pairs={{0,1},{1,0},{2,3},{3,2},{4,5},{5,4},{6,7},{7,6},{8,9},{9,8},{10,11... | collective-permute-start | bytes 110600 | tf_op jit(solution)/shard_map/ppermute | solution.py:423
  26.8 6.2 %collective-permute-start.4 = (bf16[400,128]{1,0:T(8,128)(2,1)S(1)}, bf16[400,128]{1,0:T(8,128)(2,1)S(1)}, u32[]{:S(2)}, u32[]{:S(2)}) collective-permute-start(bf16[400,128]{1,0:T(8,128)(2,1)S(1)} %get-tuple-element.57), channel_id=1, source_target_pairs={{0,16},{16,0},{1,17},{17,1},{2,18},{18,2},{3,19},{19,3},{4,20},{20... | collective-permute-start | bytes 307208 | tf_op jit(solution)/shard_map/ppermute | solution.py:429
  28.9 4.0 %collective-permute-start.7 = (bf16[144,128]{1,0:T(8,128)(2,1)S(1)}, bf16[144,128]{1,0:T(8,128)(2,1)S(1)}, u32[]{:S(2)}, u32[]{:S(2)}) collective-permute-start(bf16[144,128]{1,0:T(8,128)(2,1)S(1)} %get-tuple-element.64), channel_id=1, source_target_pairs={{0,16},{16,0},{1,17},{17,1},{2,18},{18,2},{3,19},{19,3},{4,20},{20... | collective-permute-start | bytes 110600 | tf_op jit(solution)/shard_map/ppermute | solution.py:429

commit v5 on v4

--- a/solution.py
+++ b/solution.py
@@ -50,8 +50,9 @@
         ow_ref[:, t * channels : (t + 1) * channels] = rows.astype(BF16)
 
 
-def quads(items, squash, w_ref, rw_ref, ow_ref, store, sq_s, x_s, before_a=None, before_b=None):
+def quads(items, squash, w_ref, rw_ref, ow_ref, store, sq_s, xs, before_a=None, before_b=None):
     slots, channels, members = rw_ref.shape
+    x_s, xt_s = xs
 
     def stage_a(i):
         for t in range(slots):
@@ -61,11 +62,13 @@
         predicted = dot(w_ref[...], sq_s[i])
         for t in range(slots):
             part = predicted[:, t * members : (t + 1) * members]
-            x_s[i, t * channels : (t + 1) * channels, :] = (part * rw_ref[t]).astype(BF16)
+            x = (part * rw_ref[t]).astype(BF16)
+            x_s[i, t * channels : (t + 1) * channels, :] = x
+            xt_s[i, :, t * channels : (t + 1) * channels] = x.T
 
     def stage_c(i):
         x = x_s[i]
-        left = cat([x.T, ow_ref[...]], 0)
+        left = cat([xt_s[i], ow_ref[...]], 0)
         both = dot(left, x)
         square = both[:members]
         tail = both[members:]
@@ -80,15 +83,14 @@
         store(items[i], square - row - (col - total), grad)
 
     n = len(items)
-    for i in range(n + 1):
-        if i < n:
-            if before_a is not None:
-                before_a(i)
-            stage_a(i)
-        if i:
-            if before_b is not None:
-                before_b(i - 1)
-            stage_b(i - 1)
+    for i in range(n):
+        if before_a is not None:
+            before_a(i)
+        stage_a(i)
+    for i in range(n):
+        if before_b is not None:
+            before_b(i)
+        stage_b(i)
     for i in range(n):
         stage_c(i)
 
@@ -136,14 +138,11 @@
     return grams, [rows[half + p : half + p + 1] for p in range(patches)]
 
 
-def inverse_roots(grams, grads):
-    members = grams[0].shape[0]
-    every = range(len(grams))
+def inverse_roots(shifted, norm, grads):
+    members = shifted[0].shape[0]
+    every = range(len(shifted))
     rid, cid = iotas(members)
     identity = jnp.where(rid == cid, 1.0, 0.0).astype(F32)
-    shifted = [g + (members - 1.0) * identity for g in grams]
-    square = [jnp.sum(jnp.sum(s * s, axis=0, keepdims=True), axis=1, keepdims=True) for s in shifted]
-    norm = [jnp.sqrt(s) for s in square]
     inv = [1.0 / v for v in norm]
     y = [jnp.broadcast_to(g, (8, members)) for g in grads]
 
@@ -338,14 +337,33 @@
     pack(grams, grads, msg_ref)
 
 
+def shifted_sums(loc_ref, locg_ref, msg_ref):
+    n, members = loc_ref.shape[:2]
+    rid, cid = iotas(members)
+    shift = jnp.where(rid == cid, members - 1.0, 0.0).astype(F32)
+    grams, grads = unpack(msg_ref, n)
+    shifted = [loc_ref[p] + grams[p] + shift for p in range(n)]
+    square = [jnp.sum(jnp.sum(s * s, axis=0, keepdims=True), axis=1, keepdims=True) for s in shifted]
+    return shifted, [jnp.sqrt(s) for s in square], [locg_ref[p : p + 1] + grads[p] for p in range(n)]
+
+
+def sums_kernel(loc_ref, locg_ref, msg_ref, shifted_ref, norm_ref, grad_ref):
+    shifted, norm, grads = shifted_sums(loc_ref, locg_ref, msg_ref)
+    for p in range(len(grads)):
+        shifted_ref[p] = shifted[p]
+        norm_ref[p : p + 1] = jnp.broadcast_to(norm[p], grads[p].shape)
+        grad_ref[p : p + 1] = grads[p]
+
+
 def totals(refs):
-    parts = []
-    for loc_ref, locg_ref, msg_ref in (refs[:3], refs[3:]):
-        n = loc_ref.shape[0]
-        grams, grads = unpack(msg_ref, n)
-        parts.append(([loc_ref[p] + grams[p] for p in range(n)], [locg_ref[p : p + 1] + grads[p] for p in range(n)]))
-    (gi, vi), (ge, ve) = parts
-    return ge[:1] + gi + ge[1:], ve[:1] + vi + ve[1:]
+    shifted_ref, norm_ref, grad_ref = refs[:3]
+    shifted, norm, grads = shifted_sums(*refs[3:])
+    n = shifted_ref.shape[0]
+    return (
+        shifted[:1] + [shifted_ref[p] for p in range(n)] + shifted[1:],
+        norm[:1] + [norm_ref[p : p + 1, 0:1] for p in range(n)] + norm[1:],
+        grads[:1] + [grad_ref[p : p + 1] for p in range(n)] + grads[1:],
+    )
 
 
 def root_kernel(odd_ref, *refs):
@@ -401,6 +419,12 @@
 SPACES = {"s": pltpu.SMEM, "v": pltpu.VMEM, "h": pltpu.HBM}
 
 
+def vmem_of(s):
+    if isinstance(s, list):
+        return tuple(vmem_of(e) for e in s)
+    return pltpu.VMEM(*s) if isinstance(s, tuple) else s
+
+
 def call(kernel, out_shape, args, kinds, scratch=(), flops=10 ** 9, out_kinds=None):
     outs = [jax.ShapeDtypeStruct(s, d) for s, d in out_shape]
     spec = lambda k: pl.BlockSpec(memory_space=SPACES[k])
@@ -409,7 +433,7 @@
         out_shape=outs,
         in_specs=[spec(k) for k in kinds],
         out_specs=[spec(k) for k in (out_kinds or "v" * len(outs))],
-        scratch_shapes=[pltpu.VMEM(*s) if isinstance(s, tuple) else s for s in scratch],
+        scratch_shapes=[vmem_of(s) for s in scratch],
         cost_estimate=pl.CostEstimate(flops=flops, bytes_accessed=0, transcendentals=0),
         compiler_params=pltpu.CompilerParams(vmem_limit_bytes=VMEM_LIMIT),
         name=kernel.__name__,
@@ -445,12 +469,12 @@
     inner_out = [gram(inner), grad(inner), message(inner), gram(2), grad(2)]
     inner_scratch = (
         ((inner, rows, slots * members), BF16),
-        ((inner, slots * channels, members), BF16),
+        [((inner, slots * channels, members), BF16), ((inner, members, slots * channels), BF16)],
         gram(inner),
     )
     scratch = lambda n: (
         ((n, rows, slots * members), BF16),
-        ((n, slots * channels, members), BF16),
+        [((n, slots * channels, members), BF16), ((n, members, slots * channels), BF16)],
     )
     rw = ((slots, channels, members), F32)
     ow = ((16, slots * channels), BF16)
@@ -477,7 +501,9 @@
     )
     parts = (states,)
     for step in range(OUTER):
-        sums = (*loc, over_slots(msg))
+        sums = tuple(
+            call(sums_kernel, [gram(inner), grad(inner), grad(inner)], (*loc, over_slots(msg)), "vvv", flops=10 ** 8)
+        )
         *loc, msg = call(
             combine_kernel,
             [gram(2), grad(2), message(2)],

time: 37.9 us -> 37.4 us (0.987)
  Pallas kernels: 19.6 us -> 19 us
    pallas_call x7 -> x9, Pallas kernels: 19.6 us -> 19 us  [call(): pl.pallas_call(kernel, out_shape=outs, in_specs=[spec(k) for k in kinds],...]
    ppermute x4, waiting for transfers between devices: 6.41 us -> 5.88 us  [over_slots(): return lax.ppermute(msg, 'slot', [(0, 1), (1, 0)])]
    ppermute x2, waiting for transfers between devices: 0.49 us -> 0.97 us  [neighbours(): lax.ppermute(far, 'region', cross)]
  transfers between devices with their start and end apart: 8 -> 8, of which waited for: 3 -> 5; matrix products, arithmetic and copies ran while one was open for 0% -> 0% of each run, Pallas kernels for 20% -> 19%
where the time goes in v5:
time: 37.4 us; the launch traced here: 37.2 us
  Pallas kernels  19 us (51%)
  starting transfers between devices  11.1 us (30%)
  waiting for transfers between devices  6.86 us (18%)
    pallas_call x9, Pallas kernels, call(): pl.pallas_call(kernel, out_shape=outs, in_specs=[spec(k) for k in kinds],...  19 us
    ppermute x2, starting transfers between devices, neighbours(): lax.ppermute(far, 'region', cross)  6.04 us
    ppermute x4, waiting for transfers between devices, over_slots(): return lax.ppermute(msg, 'slot', [(0, 1), (1, 0)])  5.88 us
    ppermute x4, starting transfers between devices, over_slots(): return lax.ppermute(msg, 'slot', [(0, 1), (1, 0)])  5.09 us
    ppermute x2, waiting for transfers between devices, neighbours(): lax.ppermute(far, 'region', cross)  0.97 us
  transfers between devices with their start and end apart: 8, of which 5 were waited for; matrix products, arithmetic and copies ran while one was open for 0% of the time, Pallas kernels for 19%

profile of v5, /device:TPU:0, one launch (start us, length us, event | category | flops | bytes accessed | tf_op | source)
XLA Modules:
  0.0 37.2 jit_solution(17749637451555037837)
XLA Ops:
  0.0 3.1 %first_kernel.1 = (bf16[2,8,512,128]{3,2,1,0:T(8,128)(2,1)S(1)}, bf16[1024,512]{1,0:T(8,128)(2,1)S(1)}, f32[2,128,128]{2,1,0:T(8,128)S(1)}, f32[2,128]{1,0:T(2,1...) custom-call(s32[1]{0:T(128)} %bitcast.odd_ref, ...), custom_call_target="tpu_custom_call" | custom-call | flops 1000000000 | tf_op jit(solution)/shard_map/first_kernel/pallas_call | solution.py:431
  3.1 5.5 %collective-permute-start.1 = (bf16[144,128]{1,0:T(8,128)(2,1)S(1)}, bf16[144,128]{1,0:T(8,128)(2,1)S(1)}, u32[]{:S(2)}, u32[]{:S(2)}) collective-permute-start(bf16[144,128]{1,0:T(8,128)(2,1)S(1)} %get-tuple-element.56), channel_id=1, source_target_pairs={{0,15},{1,2},{2,1},{3,4},{4,3},{5,6},{6,5},{7,8},{8,7},{9,10},{10,... | collective-permute-start | bytes 110600 | tf_op jit(solution)/shard_map/ppermute | solution.py:447
  8.6 0.0 collective-permute-start.2
  8.6 3.1 %inner_kernel.1 = (f32[6,128,128]{2,1,0:T(8,128)S(1)}, f32[6,128]{1,0:T(8,128)S(1)}, bf16[400,128]{1,0:T(8,128)(2,1)S(1)}, f32[2,128,128]{2,1,0:T(8,128)S(1)}, f32[2,128]{1,0:T(2,128)S(1)}) custom-call(bf16[2,8,512,128]{3,2,1,0:T(8,128)(2,1)S(1)} %get-tuple-element.42.states_ref.refs_6_, bf16[1024,512]{1,0:T(8,128)(2,1)S(1)} %get-tuple-element.43.w_ref.refs_7_, ...), custom_call_target="tpu_custom_call" | custom-call | flops 1000000000 | tf_op jit(solution)/shard_map/inner_kernel/pallas_call | solution.py:431
  11.7 1.6 %collective-permute-start = (bf16[400,128]{1,0:T(8,128)(2,1)S(1)}, bf16[400,128]{1,0:T(8,128)(2,1)S(1)}, u32[]{:S(2)}, u32[]{:S(2)}) collective-permute-start(bf16[400,128]{1,0:T(8,128)(2,1)S(1)} %get-tuple-element.50), channel_id=1, source_target_pairs={{0,16},{16,0},{1,17},{17,1},{2,18},{18,2},{3,19},{19,3},{4,20},{20... | collective-permute-start | bytes 307208 | tf_op jit(solution)/shard_map/ppermute | solution.py:453
  13.3 0.0 collective-permute-done.1.far_ref
  13.3 0.0 collective-permute-done.2.near_ref
  13.3 0.1 combine_kernel.2
  13.4 0.6 %collective-permute-start.3 = (bf16[144,128]{1,0:T(8,128)(2,1)S(1)}, bf16[144,128]{1,0:T(8,128)(2,1)S(1)}, u32[]{:S(2)}, u32[]{:S(2)}) collective-permute-start(bf16[144,128]{1,0:T(8,128)(2,1)S(1)} %get-tuple-element.60), channel_id=1, source_target_pairs={{0,16},{16,0},{1,17},{17,1},{2,18},{18,2},{3,19},{19,3},{4,20},{20... | collective-permute-start | bytes 110600 | tf_op jit(solution)/shard_map/ppermute | solution.py:453
  14.0 3.5 %collective-permute-done.msg_ref = bf16[400,128]{1,0:T(8,128)(2,1)S(1)} collective-permute-done((bf16[400,128]{1,0:T(8,128)(2,1)S(1)}, bf16[400,128]{1,0:T(8,128)(2,1)S(1)}, u32[]{:S(2)}, u32[]{:S(2)}) %collective-permute-start) | collective-permute-done | bytes 102432 | tf_op jit(solution)/shard_map/ppermute | solution.py:453
  17.5 0.3 sums_kernel.2
  17.7 0.1 collective-permute-done.3.refs_5_
  17.9 4.3 %root_kernel.1 = (bf16[6,128,128]{2,1,0:T(8,128)(2,1)S(1)}, bf16[2,2,512,128]{3,2,1,0:T(8,128)(2,1)S(1)}, f32[2,128,128]{2,1,0:T(8,128)S(1)}, f32[2,128]{1,0:T(2...) custom-call(s32[1]{0:T(128)} %bitcast.odd_ref, f32[6,128,128]{2,1,0:T(8,128)S(1)} %get-tuple-element.51.refs_0_, ...), custom_call_target="tpu_custom_call" | custom-call | flops 1000000000 | tf_op jit(solution)/shard_map/root_kernel/pallas_call | solution.py:431
  22.2 0.5 %collective-permute-start.5 = (bf16[144,128]{1,0:T(8,128)(2,1)S(1)}, bf16[144,128]{1,0:T(8,128)(2,1)S(1)}, u32[]{:S(2)}, u32[]{:S(2)}) collective-permute-start(bf16[144,128]{1,0:T(8,128)(2,1)S(1)} %get-tuple-element.72), channel_id=1, source_target_pairs={{0,15},{1,2},{2,1},{3,4},{4,3},{5,6},{6,5},{7,8},{8,7},{9,10},{10,... | collective-permute-start | bytes 110600 | tf_op jit(solution)/shard_map/ppermute | solution.py:447
  22.7 0.0 collective-permute-start.6
  22.7 3.3 %advance_kernel.1 = (bf16[2,6,512,128]{3,2,1,0:T(8,128)(2,1)S(1)}, f32[6,128,128]{2,1,0:T(8,128)S(1)}, f32[6,128]{1,0:T(8,128)S(1)}, bf16[400,128]{1,0:T(8,128)(...) custom-call(bf16[6,128,128]{2,1,0:T(8,128)(2,1)S(1)} %get-tuple-element.61.mix_ref, ...), custom_call_target="tpu_custom_call" | custom-call | flops 1000000000 | tf_op jit(solution)/shard_map/advance_kernel/pallas_call | solution.py:431
  26.0 1.4 %collective-permute-start.4 = (bf16[400,128]{1,0:T(8,128)(2,1)S(1)}, bf16[400,128]{1,0:T(8,128)(2,1)S(1)}, u32[]{:S(2)}, u32[]{:S(2)}) collective-permute-start(bf16[400,128]{1,0:T(8,128)(2,1)S(1)} %get-tuple-element.66), channel_id=1, source_target_pairs={{0,16},{16,0},{1,17},{17,1},{2,18},{18,2},{3,19},{19,3},{4,20},{20... | collective-permute-start | bytes 307208 | tf_op jit(solution)/shard_map/ppermute | solution.py:453
  27.4 1.0 %collective-permute-done.5.far_ref = bf16[144,128]{1,0:T(8,128)(2,1)S(1)} collective-permute-done((bf16[144,128]{1,0:T(8,128)(2,1)S(1)}, bf16[144,128]{1,0:T(8,128)(2,1)S(1)}, u32[]{:S(2)}, u32[]{:S(2)}) %collective-permute-start.5) | collective-permute-done | bytes 36896 | tf_op jit(solution)/shard_map/ppermute | solution.py:447
  28.4 0.1 combine_kernel.3
  28.4 1.6 %collective-permute-start.7 = (bf16[144,128]{1,0:T(8,128)(2,1)S(1)}, bf16[144,128]{1,0:T(8,128)(2,1)S(1)}, u32[]{:S(2)}, u32[]{:S(2)}) collective-permute-start(bf16[144,128]{1,0:T(8,128)(2,1)S(1)} %get-tuple-element.76), channel_id=1, source_target_pairs={{0,16},{16,0},{1,17},{17,1},{2,18},{18,2},{3,19},{19,3},{4,20},{20... | collective-permute-start | bytes 110600 | tf_op jit(solution)/shard_map/ppermute | solution.py:453
  30.0 1.8 %collective-permute-done.4.msg_ref = bf16[400,128]{1,0:T(8,128)(2,1)S(1)} collective-permute-done((bf16[400,128]{1,0:T(8,128)(2,1)S(1)}, bf16[400,128]{1,0:T(8,128)(2,1)S(1)}, u32[]{:S(2)}, u32[]{:S(2)}) %collective-permute-start.4) | collective-permute-done | bytes 102432 | tf_op jit(solution)/shard_map/ppermute | solution.py:453
  31.8 0.3 sums_kernel.3
  32.0 0.4 %collective-permute-done.7.refs_5_ = bf16[144,128]{1,0:T(8,128)(2,1)S(1)} collective-permute-done((bf16[144,128]{1,0:T(8,128)(2,1)S(1)}, bf16[144,128]{1,0:T(8,128)(2,1)S(1)}, u32[]{:S(2)}, u32[]{:S(2)}) %collective-permute-start.7) | collective-permute-done | bytes 36896 | tf_op jit(solution)/shard_map/ppermute | solution.py:453
  32.4 4.6 %last_kernel.1 = bf16[2,8,512,128]{3,2,1,0:T(8,128)(2,1)} custom-call(f32[6,128,128]{2,1,0:T(8,128)S(1)} %get-tuple-element.67.refs_0_, f32[6,128]{1,0:T(8,128)S(1)} %get-tuple-element.68.refs_1_, f32[6,128]{1,0:T(8,128)S(1)} %get-tuple-element.69.refs_2_, f32[2,128,128]{2,1,0:T(8,128)S(1)} %get-tuple-element.74.refs_3_, ...), custom_call_target="tpu_custom_call" | custom-call | flops 1000000000 | tf_op jit(solution)/shard_map/last_kernel/pallas_call | solution.py:431
  (1 shorter events, 0.0 us)
Async XLA Ops:
  3.1 10.2 %collective-permute-start.1 = (bf16[144,128]{1,0:T(8,128)(2,1)S(1)}, bf16[144,128]{1,0:T(8,128)(2,1)S(1)}, u32[]{:S(2)}, u32[]{:S(2)}) collective-permute-start(bf16[144,128]{1,0:T(8,128)(2,1)S(1)} %get-tuple-element.56), channel_id=1, source_target_pairs={{0,15},{1,2},{2,1},{3,4},{4,3},{5,6},{6,5},{7,8},{8,7},{9,10},{10,... | collective-permute-start | bytes 110600 | tf_op jit(solution)/shard_map/ppermute | solution.py:447
  8.6 4.7 %collective-permute-start.2 = (bf16[144,128]{1,0:T(8,128)(2,1)S(1)}, bf16[144,128]{1,0:T(8,128)(2,1)S(1)}, u32[]{:S(2)}, u32[]{:S(2)}) collective-permute-start(bf16[144,128]{1,0:T(8,128)(2,1)S(1)} %get-tuple-element.57), channel_id=1, source_target_pairs={{0,1},{1,0},{2,3},{3,2},{4,5},{5,4},{6,7},{7,6},{8,9},{9,8},{10,11... | collective-permute-start | bytes 110600 | tf_op jit(solution)/shard_map/ppermute | solution.py:447
  11.7 5.8 %collective-permute-start = (bf16[400,128]{1,0:T(8,128)(2,1)S(1)}, bf16[400,128]{1,0:T(8,128)(2,1)S(1)}, u32[]{:S(2)}, u32[]{:S(2)}) collective-permute-start(bf16[400,128]{1,0:T(8,128)(2,1)S(1)} %get-tuple-element.50), channel_id=1, source_target_pairs={{0,16},{16,0},{1,17},{17,1},{2,18},{18,2},{3,19},{19,3},{4,20},{20... | collective-permute-start | bytes 307208 | tf_op jit(solution)/shard_map/ppermute | solution.py:453
  13.4 4.5 %collective-permute-start.3 = (bf16[144,128]{1,0:T(8,128)(2,1)S(1)}, bf16[144,128]{1,0:T(8,128)(2,1)S(1)}, u32[]{:S(2)}, u32[]{:S(2)}) collective-permute-start(bf16[144,128]{1,0:T(8,128)(2,1)S(1)} %get-tuple-element.60), channel_id=1, source_target_pairs={{0,16},{16,0},{1,17},{17,1},{2,18},{18,2},{3,19},{19,3},{4,20},{20... | collective-permute-start | bytes 110600 | tf_op jit(solution)/shard_map/ppermute | solution.py:453
  22.2 6.1 %collective-permute-start.5 = (bf16[144,128]{1,0:T(8,128)(2,1)S(1)}, bf16[144,128]{1,0:T(8,128)(2,1)S(1)}, u32[]{:S(2)}, u32[]{:S(2)}) collective-permute-start(bf16[144,128]{1,0:T(8,128)(2,1)S(1)} %get-tuple-element.72), channel_id=1, source_target_pairs={{0,15},{1,2},{2,1},{3,4},{4,3},{5,6},{6,5},{7,8},{8,7},{9,10},{10,... | collective-permute-start | bytes 110600 | tf_op jit(solution)/shard_map/ppermute | solution.py:447
  22.7 5.6 %collective-permute-start.6 = (bf16[144,128]{1,0:T(8,128)(2,1)S(1)}, bf16[144,128]{1,0:T(8,128)(2,1)S(1)}, u32[]{:S(2)}, u32[]{:S(2)}) collective-permute-start(bf16[144,128]{1,0:T(8,128)(2,1)S(1)} %get-tuple-element.73), channel_id=1, source_target_pairs={{0,1},{1,0},{2,3},{3,2},{4,5},{5,4},{6,7},{7,6},{8,9},{9,8},{10,11... | collective-permute-start | bytes 110600 | tf_op jit(solution)/shard_map/ppermute | solution.py:447
  26.0 5.8 %collective-permute-start.4 = (bf16[400,128]{1,0:T(8,128)(2,1)S(1)}, bf16[400,128]{1,0:T(8,128)(2,1)S(1)}, u32[]{:S(2)}, u32[]{:S(2)}) collective-permute-start(bf16[400,128]{1,0:T(8,128)(2,1)S(1)} %get-tuple-element.66), channel_id=1, source_target_pairs={{0,16},{16,0},{1,17},{17,1},{2,18},{18,2},{3,19},{19,3},{4,20},{20... | collective-permute-start | bytes 307208 | tf_op jit(solution)/shard_map/ppermute | solution.py:453
  28.4 4.0 %collective-permute-start.7 = (bf16[144,128]{1,0:T(8,128)(2,1)S(1)}, bf16[144,128]{1,0:T(8,128)(2,1)S(1)}, u32[]{:S(2)}, u32[]{:S(2)}) collective-permute-start(bf16[144,128]{1,0:T(8,128)(2,1)S(1)} %get-tuple-element.76), channel_id=1, source_target_pairs={{0,16},{16,0},{1,17},{17,1},{2,18},{18,2},{3,19},{19,3},{4,20},{20... | collective-permute-start | bytes 110600 | tf_op jit(solution)/shard_map/ppermute | solution.py:453

commit v6 on v5

--- a/solution.py
+++ b/solution.py
@@ -146,12 +146,9 @@
     inv = [1.0 / v for v in norm]
     y = [jnp.broadcast_to(g, (8, members)) for g in grads]
 
-    def with_row(mat, row):
+    def tile(row):
         high = row.astype(BF16).astype(F32)
-        return cat([mat, cat([high, row - high], 0).astype(BF16)], 0)
-
-    def row_of(prod):
-        return prod[members : members + 8, :members] + prod[members + 8 :, :members]
+        return cat([high, row - high], 0).astype(BF16)
 
     def in_pairs(left, right):
         out = []
@@ -162,35 +159,47 @@
             out += [prod[:, :members], prod[:, members:]]
         return out
 
+    def times(right, parts):
+        prod = in_pairs([cat(rows, 0) for rows in zip(*parts)], right)
+        at, found = 0, []
+        for part in parts:
+            size = part[0].shape[0]
+            found.append([v[at : at + size] for v in prod])
+            at += size
+        return found
+
     z = [None for _ in every]
     for step in range(NS_SPLIT):
+        rows = [tile(v) for v in y]
         if step == 0:
             th = [v.astype(BF16) for v in shifted]
-            prod = [dot(with_row(th[i], y[i]), th[i]) * inv[i] for i in every]
+            square, row = times(th, [th, rows])
             t = [shifted[i] * inv[i] for i in every]
-            square = [prod[i][:members] * inv[i] for i in every]
+            square = [square[i] * (inv[i] * inv[i]) for i in every]
+            row = [row[i] * inv[i] for i in every]
             z = [1.5 * identity - 0.5 * v for v in t]
         else:
             th = [v.astype(BF16) for v in t]
-            prod = [dot(with_row(th[i], y[i]), cat([th[i], z[i].astype(BF16)], 1)) for i in every]
-            square = [v[:members, :members] for v in prod]
-            z = [1.5 * z[i] - 0.5 * prod[i][:members, members:] for i in every]
-        y = [1.5 * y[i] - 0.5 * row_of(prod[i]) for i in every]
-        x = [(1.5 * t[i] - 0.25 * square[i]).astype(BF16) for i in every]
-        shrunk = in_pairs(x, th)
+            square, row, moved = times(th, [th, rows, [v.astype(BF16) for v in z]])
+            z = [1.5 * z[i] - 0.5 * moved[i] for i in every]
+        y = [1.5 * y[i] - 0.5 * (row[i][:8] + row[i][8:]) for i in every]
+        shrunk = in_pairs([(1.5 * t[i] - 0.25 * square[i]).astype(BF16) for i in every], th)
         if step == 0:
             shrunk = [shrunk[i] * inv[i] for i in every]
         t = [2.25 * t[i] - shrunk[i] for i in every]
     d = [identity - v for v in t]
     for step in range(NS_SPLIT, NS_STEPS):
         dh = [v.astype(BF16) for v in d]
-        prod = [dot(with_row(dh[i], y[i]), cat([dh[i], z[i].astype(BF16)], 1)) for i in every]
-        z = [z[i] + 0.5 * prod[i][:members, members:] for i in every]
-        y = [y[i] + 0.5 * row_of(prod[i]) for i in every]
+        rows = [tile(v) for v in y]
+        zh = [v.astype(BF16) for v in z]
         if step < NS_STEPS - 1:
-            d2 = [v[:members, :members] for v in prod]
-            d3 = in_pairs([v.astype(BF16) for v in d2], dh)
-            d = [0.75 * d2[i] + 0.25 * d3[i] for i in every]
+            square, row, moved = times(dh, [dh, rows, zh])
+            cube = in_pairs([v.astype(BF16) for v in square], dh)
+            d = [0.75 * square[i] + 0.25 * cube[i] for i in every]
+        else:
+            row, moved = times(dh, [rows, zh])
+        z = [z[i] + 0.5 * moved[i] for i in every]
+        y = [y[i] + 0.5 * (row[i][:8] + row[i][8:]) for i in every]
 
     scale = math.sqrt(members - 1.0)
     share = 1.0 / members
@@ -211,11 +220,21 @@
     return lambda p, t: jnp.tanh(states_ref[t, p].astype(F32)).astype(BF16)
 
 
+def move(parts, mixing):
+    moved = dot_nt(cat(parts, 0), mixing).astype(BF16)
+    rows = parts[0].shape[0]
+    return [moved[k * rows : (k + 1) * rows] for k in range(len(parts))]
+
+
 def advance(states_ref, mixing_of, new_ref):
+    slots = states_ref.shape[0]
+    fresh = {}
+
     def squash(p, t):
-        fresh = dot_nt(states_ref[t, p], mixing_of(p)).astype(BF16)
-        new_ref[t, p] = fresh
-        return jnp.tanh(fresh.astype(F32)).astype(BF16)
+        if p not in fresh:
+            fresh[p] = move([states_ref[k, p] for k in range(slots)], mixing_of(p))
+        new_ref[t, p] = fresh[p][t]
+        return jnp.tanh(fresh[p][t].astype(F32)).astype(BF16)
 
     return squash
 
@@ -401,15 +420,17 @@
     mixing = [m.astype(BF16) for m in inverse_roots(*totals(refs[:6]))]
     slots, patches = out_s.shape[:2]
     copies = []
+
+    def value(t, p):
+        if len(states) == 1:
+            return states[0][t, p]
+        if p in (0, patches - 1):
+            return states[0][t, min(p, 1)]
+        return states[1][t, p - 1]
+
     for p in range(patches):
-        for t in range(slots):
-            if len(states) == 1:
-                value = states[0][t, p]
-            elif p in (0, patches - 1):
-                value = states[0][t, min(p, 1)]
-            else:
-                value = states[1][t, p - 1]
-            out_s[t, p] = dot_nt(value, mixing[p]).astype(BF16)
+        for t, fresh in enumerate(move([value(t, p) for t in range(slots)], mixing[p])):
+            out_s[t, p] = fresh
             copies.append(pltpu.make_async_copy(out_s.at[t, p], out_hbm.at[t, p], sems.at[len(copies)]))
             copies[-1].start()
     for c in copies:

time: 37.4 us -> 36.9 us (0.987)
  transfers between devices with their start and end apart: 8 -> 8, of which waited for: 5 -> 5; matrix products, arithmetic and copies ran while one was open for 0% -> 0% of each run, Pallas kernels for 19% -> 20%
where the time goes in v6:
time: 36.9 us; the launch traced here: 36.8 us
  Pallas kernels  18.8 us (51%)
  starting transfers between devices  11.1 us (30%)
  waiting for transfers between devices  6.68 us (18%)
    pallas_call x9, Pallas kernels, call(): pl.pallas_call(kernel, out_shape=outs, in_specs=[spec(k) for k in kinds],...  18.8 us
    ppermute x2, starting transfers between devices, neighbours(): lax.ppermute(far, 'region', cross)  6.04 us
    ppermute x4, waiting for transfers between devices, over_slots(): return lax.ppermute(msg, 'slot', [(0, 1), (1, 0)])  5.7 us
    ppermute x4, starting transfers between devices, over_slots(): return lax.ppermute(msg, 'slot', [(0, 1), (1, 0)])  5.09 us
    ppermute x2, waiting for transfers between devices, neighbours(): lax.ppermute(far, 'region', cross)  0.98 us
  transfers between devices with their start and end apart: 8, of which 5 were waited for; matrix products, arithmetic and copies ran while one was open for 0% of the time, Pallas kernels for 20%

profile of v6, /device:TPU:0, one launch (start us, length us, event | category | flops | bytes accessed | tf_op | source)
XLA Modules:
  0.0 36.8 jit_solution(8745908251696304076)
XLA Ops:
  0.0 3.1 %first_kernel.1 = (bf16[2,8,512,128]{3,2,1,0:T(8,128)(2,1)S(1)}, bf16[1024,512]{1,0:T(8,128)(2,1)S(1)}, f32[2,128,128]{2,1,0:T(8,128)S(1)}, f32[2,128]{1,0:T(2,1...) custom-call(s32[1]{0:T(128)} %bitcast.odd_ref, ...), custom_call_target="tpu_custom_call" | custom-call | flops 1000000000 | tf_op jit(solution)/shard_map/first_kernel/pallas_call | solution.py:452
  3.1 5.5 %collective-permute-start.1 = (bf16[144,128]{1,0:T(8,128)(2,1)S(1)}, bf16[144,128]{1,0:T(8,128)(2,1)S(1)}, u32[]{:S(2)}, u32[]{:S(2)}) collective-permute-start(bf16[144,128]{1,0:T(8,128)(2,1)S(1)} %get-tuple-element.56), channel_id=1, source_target_pairs={{0,15},{1,2},{2,1},{3,4},{4,3},{5,6},{6,5},{7,8},{8,7},{9,10},{10,... | collective-permute-start | bytes 110600 | tf_op jit(solution)/shard_map/ppermute | solution.py:468
  8.6 0.0 collective-permute-start.2
  8.6 3.1 %inner_kernel.1 = (f32[6,128,128]{2,1,0:T(8,128)S(1)}, f32[6,128]{1,0:T(8,128)S(1)}, bf16[400,128]{1,0:T(8,128)(2,1)S(1)}, f32[2,128,128]{2,1,0:T(8,128)S(1)}, f32[2,128]{1,0:T(2,128)S(1)}) custom-call(bf16[2,8,512,128]{3,2,1,0:T(8,128)(2,1)S(1)} %get-tuple-element.42.states_ref.refs_6_, bf16[1024,512]{1,0:T(8,128)(2,1)S(1)} %get-tuple-element.43.w_ref.refs_7_, ...), custom_call_target="tpu_custom_call" | custom-call | flops 1000000000 | tf_op jit(solution)/shard_map/inner_kernel/pallas_call | solution.py:452
  11.7 1.6 %collective-permute-start = (bf16[400,128]{1,0:T(8,128)(2,1)S(1)}, bf16[400,128]{1,0:T(8,128)(2,1)S(1)}, u32[]{:S(2)}, u32[]{:S(2)}) collective-permute-start(bf16[400,128]{1,0:T(8,128)(2,1)S(1)} %get-tuple-element.50), channel_id=1, source_target_pairs={{0,16},{16,0},{1,17},{17,1},{2,18},{18,2},{3,19},{19,3},{4,20},{20... | collective-permute-start | bytes 307208 | tf_op jit(solution)/shard_map/ppermute | solution.py:474
  13.3 0.0 collective-permute-done.1.far_ref
  13.3 0.1 combine_kernel.2
  13.4 0.6 %collective-permute-start.3 = (bf16[144,128]{1,0:T(8,128)(2,1)S(1)}, bf16[144,128]{1,0:T(8,128)(2,1)S(1)}, u32[]{:S(2)}, u32[]{:S(2)}) collective-permute-start(bf16[144,128]{1,0:T(8,128)(2,1)S(1)} %get-tuple-element.60), channel_id=1, source_target_pairs={{0,16},{16,0},{1,17},{17,1},{2,18},{18,2},{3,19},{19,3},{4,20},{20... | collective-permute-start | bytes 110600 | tf_op jit(solution)/shard_map/ppermute | solution.py:474
  14.0 3.5 %collective-permute-done.msg_ref = bf16[400,128]{1,0:T(8,128)(2,1)S(1)} collective-permute-done((bf16[400,128]{1,0:T(8,128)(2,1)S(1)}, bf16[400,128]{1,0:T(8,128)(2,1)S(1)}, u32[]{:S(2)}, u32[]{:S(2)}) %collective-permute-start) | collective-permute-done | bytes 102432 | tf_op jit(solution)/shard_map/ppermute | solution.py:474
  17.5 0.3 sums_kernel.2
  17.7 0.1 collective-permute-done.3.refs_5_
  17.9 4.2 %root_kernel.1 = (bf16[6,128,128]{2,1,0:T(8,128)(2,1)S(1)}, bf16[2,2,512,128]{3,2,1,0:T(8,128)(2,1)S(1)}, f32[2,128,128]{2,1,0:T(8,128)S(1)}, f32[2,128]{1,0:T(2...) custom-call(s32[1]{0:T(128)} %bitcast.odd_ref, f32[6,128,128]{2,1,0:T(8,128)S(1)} %get-tuple-element.51.refs_0_, ...), custom_call_target="tpu_custom_call" | custom-call | flops 1000000000 | tf_op jit(solution)/shard_map/root_kernel/pallas_call | solution.py:452
  22.1 0.5 %collective-permute-start.5 = (bf16[144,128]{1,0:T(8,128)(2,1)S(1)}, bf16[144,128]{1,0:T(8,128)(2,1)S(1)}, u32[]{:S(2)}, u32[]{:S(2)}) collective-permute-start(bf16[144,128]{1,0:T(8,128)(2,1)S(1)} %get-tuple-element.72), channel_id=1, source_target_pairs={{0,15},{1,2},{2,1},{3,4},{4,3},{5,6},{6,5},{7,8},{8,7},{9,10},{10,... | collective-permute-start | bytes 110600 | tf_op jit(solution)/shard_map/ppermute | solution.py:468
  22.6 0.0 collective-permute-start.6
  22.6 3.3 %advance_kernel.1 = (bf16[2,6,512,128]{3,2,1,0:T(8,128)(2,1)S(1)}, f32[6,128,128]{2,1,0:T(8,128)S(1)}, f32[6,128]{1,0:T(8,128)S(1)}, bf16[400,128]{1,0:T(8,128)(...) custom-call(bf16[6,128,128]{2,1,0:T(8,128)(2,1)S(1)} %get-tuple-element.61.mix_ref, ...), custom_call_target="tpu_custom_call" | custom-call | flops 1000000000 | tf_op jit(solution)/shard_map/advance_kernel/pallas_call | solution.py:452
  25.9 1.4 %collective-permute-start.4 = (bf16[400,128]{1,0:T(8,128)(2,1)S(1)}, bf16[400,128]{1,0:T(8,128)(2,1)S(1)}, u32[]{:S(2)}, u32[]{:S(2)}) collective-permute-start(bf16[400,128]{1,0:T(8,128)(2,1)S(1)} %get-tuple-element.66), channel_id=1, source_target_pairs={{0,16},{16,0},{1,17},{17,1},{2,18},{18,2},{3,19},{19,3},{4,20},{20... | collective-permute-start | bytes 307208 | tf_op jit(solution)/shard_map/ppermute | solution.py:474
  27.3 1.0 %collective-permute-done.5.far_ref = bf16[144,128]{1,0:T(8,128)(2,1)S(1)} collective-permute-done((bf16[144,128]{1,0:T(8,128)(2,1)S(1)}, bf16[144,128]{1,0:T(8,128)(2,1)S(1)}, u32[]{:S(2)}, u32[]{:S(2)}) %collective-permute-start.5) | collective-permute-done | bytes 36896 | tf_op jit(solution)/shard_map/ppermute | solution.py:468
  28.2 0.0 collective-permute-done.6.near_ref
  28.2 0.1 combine_kernel.3
  28.3 1.6 %collective-permute-start.7 = (bf16[144,128]{1,0:T(8,128)(2,1)S(1)}, bf16[144,128]{1,0:T(8,128)(2,1)S(1)}, u32[]{:S(2)}, u32[]{:S(2)}) collective-permute-start(bf16[144,128]{1,0:T(8,128)(2,1)S(1)} %get-tuple-element.76), channel_id=1, source_target_pairs={{0,16},{16,0},{1,17},{17,1},{2,18},{18,2},{3,19},{19,3},{4,20},{20... | collective-permute-start | bytes 110600 | tf_op jit(solution)/shard_map/ppermute | solution.py:474
  29.9 1.8 %collective-permute-done.4.msg_ref = bf16[400,128]{1,0:T(8,128)(2,1)S(1)} collective-permute-done((bf16[400,128]{1,0:T(8,128)(2,1)S(1)}, bf16[400,128]{1,0:T(8,128)(2,1)S(1)}, u32[]{:S(2)}, u32[]{:S(2)}) %collective-permute-start.4) | collective-permute-done | bytes 102432 | tf_op jit(solution)/shard_map/ppermute | solution.py:474
  31.6 0.4 %sums_kernel.3 = (f32[6,128,128]{2,1,0:T(8,128)S(1)}, f32[6,128]{1,0:T(8,128)S(1)}, f32[6,128]{1,0:T(8,128)S(1)}) custom-call(f32[6,128,128]{2,1,0:T(8,128)S(1)} %get-tuple-element.64.loc_ref, f32[6,128]{1,0:T(8,128)S(1)} %get-tuple-element.65.locg_ref, bf16[400,128]{1,0:T(8,128)(2,1)S(1)} %collective-permute-done.4.msg_ref), custom_call_target="tpu_custom_call" | custom-call | flops 100000000 | tf_op jit(solution)/shard_map/sums_kernel/pallas_call | solution.py:452
  32.1 0.3 collective-permute-done.7.refs_5_
  32.3 4.3 %last_kernel.1 = bf16[2,8,512,128]{3,2,1,0:T(8,128)(2,1)} custom-call(f32[6,128,128]{2,1,0:T(8,128)S(1)} %get-tuple-element.67.refs_0_, f32[6,128]{1,0:T(8,128)S(1)} %get-tuple-element.68.refs_1_, f32[6,128]{1,0:T(8,128)S(1)} %get-tuple-element.69.refs_2_, f32[2,128,128]{2,1,0:T(8,128)S(1)} %get-tuple-element.74.refs_3_, ...), custom_call_target="tpu_custom_call" | custom-call | flops 1000000000 | tf_op jit(solution)/shard_map/last_kernel/pallas_call | solution.py:452
  (1 shorter events, 0.0 us)
Async XLA Ops:
  3.1 10.2 %collective-permute-start.1 = (bf16[144,128]{1,0:T(8,128)(2,1)S(1)}, bf16[144,128]{1,0:T(8,128)(2,1)S(1)}, u32[]{:S(2)}, u32[]{:S(2)}) collective-permute-start(bf16[144,128]{1,0:T(8,128)(2,1)S(1)} %get-tuple-element.56), channel_id=1, source_target_pairs={{0,15},{1,2},{2,1},{3,4},{4,3},{5,6},{6,5},{7,8},{8,7},{9,10},{10,... | collective-permute-start | bytes 110600 | tf_op jit(solution)/shard_map/ppermute | solution.py:468
  8.6 4.7 %collective-permute-start.2 = (bf16[144,128]{1,0:T(8,128)(2,1)S(1)}, bf16[144,128]{1,0:T(8,128)(2,1)S(1)}, u32[]{:S(2)}, u32[]{:S(2)}) collective-permute-start(bf16[144,128]{1,0:T(8,128)(2,1)S(1)} %get-tuple-element.57), channel_id=1, source_target_pairs={{0,1},{1,0},{2,3},{3,2},{4,5},{5,4},{6,7},{7,6},{8,9},{9,8},{10,11... | collective-permute-start | bytes 110600 | tf_op jit(solution)/shard_map/ppermute | solution.py:468
  11.7 5.8 %collective-permute-start = (bf16[400,128]{1,0:T(8,128)(2,1)S(1)}, bf16[400,128]{1,0:T(8,128)(2,1)S(1)}, u32[]{:S(2)}, u32[]{:S(2)}) collective-permute-start(bf16[400,128]{1,0:T(8,128)(2,1)S(1)} %get-tuple-element.50), channel_id=1, source_target_pairs={{0,16},{16,0},{1,17},{17,1},{2,18},{18,2},{3,19},{19,3},{4,20},{20... | collective-permute-start | bytes 307208 | tf_op jit(solution)/shard_map/ppermute | solution.py:474
  13.4 4.5 %collective-permute-start.3 = (bf16[144,128]{1,0:T(8,128)(2,1)S(1)}, bf16[144,128]{1,0:T(8,128)(2,1)S(1)}, u32[]{:S(2)}, u32[]{:S(2)}) collective-permute-start(bf16[144,128]{1,0:T(8,128)(2,1)S(1)} %get-tuple-element.60), channel_id=1, source_target_pairs={{0,16},{16,0},{1,17},{17,1},{2,18},{18,2},{3,19},{19,3},{4,20},{20... | collective-permute-start | bytes 110600 | tf_op jit(solution)/shard_map/ppermute | solution.py:474
  22.1 6.1 %collective-permute-start.5 = (bf16[144,128]{1,0:T(8,128)(2,1)S(1)}, bf16[144,128]{1,0:T(8,128)(2,1)S(1)}, u32[]{:S(2)}, u32[]{:S(2)}) collective-permute-start(bf16[144,128]{1,0:T(8,128)(2,1)S(1)} %get-tuple-element.72), channel_id=1, source_target_pairs={{0,15},{1,2},{2,1},{3,4},{4,3},{5,6},{6,5},{7,8},{8,7},{9,10},{10,... | collective-permute-start | bytes 110600 | tf_op jit(solution)/shard_map/ppermute | solution.py:468
  22.6 5.6 %collective-permute-start.6 = (bf16[144,128]{1,0:T(8,128)(2,1)S(1)}, bf16[144,128]{1,0:T(8,128)(2,1)S(1)}, u32[]{:S(2)}, u32[]{:S(2)}) collective-permute-start(bf16[144,128]{1,0:T(8,128)(2,1)S(1)} %get-tuple-element.73), channel_id=1, source_target_pairs={{0,1},{1,0},{2,3},{3,2},{4,5},{5,4},{6,7},{7,6},{8,9},{9,8},{10,11... | collective-permute-start | bytes 110600 | tf_op jit(solution)/shard_map/ppermute | solution.py:468
  25.9 5.8 %collective-permute-start.4 = (bf16[400,128]{1,0:T(8,128)(2,1)S(1)}, bf16[400,128]{1,0:T(8,128)(2,1)S(1)}, u32[]{:S(2)}, u32[]{:S(2)}) collective-permute-start(bf16[400,128]{1,0:T(8,128)(2,1)S(1)} %get-tuple-element.66), channel_id=1, source_target_pairs={{0,16},{16,0},{1,17},{17,1},{2,18},{18,2},{3,19},{19,3},{4,20},{20... | collective-permute-start | bytes 307208 | tf_op jit(solution)/shard_map/ppermute | solution.py:474
  28.3 4.0 %collective-permute-start.7 = (bf16[144,128]{1,0:T(8,128)(2,1)S(1)}, bf16[144,128]{1,0:T(8,128)(2,1)S(1)}, u32[]{:S(2)}, u32[]{:S(2)}) collective-permute-start(bf16[144,128]{1,0:T(8,128)(2,1)S(1)} %get-tuple-element.76), channel_id=1, source_target_pairs={{0,16},{16,0},{1,17},{17,1},{2,18},{18,2},{3,19},{19,3},{4,20},{20... | collective-permute-start | bytes 110600 | tf_op jit(solution)/shard_map/ppermute | solution.py:474
